TPU v7x, 16 devices: a whole 2x2x2 slice. The times are simulated.
16 devices in a mesh: col: 2 (over z), row: 8 (over y, x, core).
Axes of the slice: x: 2, y: 2, z: 2, core: 2. Of those that a mesh axis runs over, the one named last changes fastest.
Arguments:
- vel_u: float32 [20, 1024, 1024], P(None, 'row', 'col')
- vel_v: float32 [20, 1024, 1024], P(None, 'row', 'col')
- temperature: float32 [20, 1024, 1024], P(None, 'row', 'col')
- salinity: float32 [20, 1024, 1024], P(None, 'row', 'col')
- sea_level: float32 [1024, 1024], P('row', 'col')
- trans_u: float32 [1024, 1024], P('row', 'col')
- trans_v: float32 [1024, 1024], P('row', 'col')
- bathymetry: float32 [1024, 1024], P('row', 'col')
- kmt_levels: int32 [1024, 1024], P('row', 'col')
- tide_force: float32 [20, 2], replicated
Outputs:
- output 1: float32 [1024, 1024], P('row', 'col')
- output 2: float32 [1024, 1024], P('row', 'col')
- output 3: float32 [1024, 1024], P('row', 'col')
- output 4: float32 [20, 1024, 1024], P(None, 'row', 'col')
- output 5: float32 [20, 1024, 1024], P(None, 'row', 'col')
- output 6: float32 [20, 1024, 1024], P(None, 'row', 'col')
- output 7: float32 [20, 1024, 1024], P(None, 'row', 'col')
All inputs are finite; a program needn't handle non-finite values.
Results may differ from a plain program's by a relative error of at most 0.001.
Values sent between devices are 32-bit elements.
A program may use at most 1 GiB of HBM per device.

v0:
```python
import jax
import jax.numpy as jnp
from jax import lax
from jax.sharding import PartitionSpec as P

GRAVITY = 1.0
GRID_DX = 1.0
TIME_STEP = 4.0
ALPHA_T = 0.02
BETA_S = 0.015
T_REF = 1.0
S_REF = 1.0
VISC_KV = 0.001
DIFF_KT = 0.0005


def level_mask(count, n_levels):
    levels = jnp.arange(n_levels, dtype=jnp.int32)[:, None, None]
    return (levels < count[None]).astype(jnp.float32)


def interface_coef(count, thick, kappa, n_levels):
    levels = jnp.arange(n_levels - 1, dtype=jnp.int32)[:, None, None]
    active = (levels + 1 < count[None]).astype(jnp.float32)
    safe = jnp.where(count > 0, thick, 1.0)
    return active * (TIME_STEP * kappa / (safe * safe))[None]


def column_solve(source, couple):
    edge = jnp.zeros_like(source[:1])
    upper = jnp.concatenate([couple, edge], axis=0)
    lower = jnp.concatenate([edge, couple], axis=0)
    diag = 1.0 + upper + lower

    def forward(carry, slab):
        gain_prev, part_prev = carry
        lower_k, diag_k, upper_k, source_k = slab
        pivot = diag_k - lower_k * gain_prev
        gain = upper_k / pivot
        part = (source_k + lower_k * part_prev) / pivot
        return (gain, part), (gain, part)

    start = (jnp.zeros_like(source[0]), jnp.zeros_like(source[0]))
    _, (gains, parts) = lax.scan(forward, start, (lower, diag, upper, source))

    def backward(below, slab):
        gain, part = slab
        here = part + gain * below
        return here, here

    _, profile = lax.scan(backward, jnp.zeros_like(source[0]), (gains, parts), reverse=True)
    return profile


def geometry(kmt_ext, depth_ext):
    kmt_cell = kmt_ext[1:-1, 1:-1]
    thick_ext = depth_ext / jnp.maximum(kmt_ext, 1).astype(jnp.float32)
    thick_cell = thick_ext[1:-1, 1:-1]
    return {"k_cell": kmt_cell, "k_u": jnp.minimum(kmt_cell, kmt_ext[1:-1, 2:]), "k_v": jnp.minimum(kmt_cell, kmt_ext[2:, 1:-1]), "dz_cell": thick_cell, "dz_u": 0.5 * (thick_cell + thick_ext[1:-1, 2:]), "dz_v": 0.5 * (thick_cell + thick_ext[2:, 1:-1])}


def surface_fields(layout):
    k_faces = jnp.stack([layout["k_u"], layout["k_v"]])
    face_depth = k_faces.astype(jnp.float32) * jnp.stack([layout["dz_u"], layout["dz_v"]])
    face_wet = (k_faces > 0).astype(jnp.float32)
    wet_cell = (layout["k_cell"] > 0).astype(jnp.float32)
    return face_depth, face_wet, wet_cell


def momentum_tend(u_ext, v_ext, p_ext):
    cen_u = 0.5 * (u_ext[:, 1:-1, :-1] + u_ext[:, 1:-1, 1:])
    corner_v = 0.5 * (v_ext[:, :-1, 1:-1] + v_ext[:, :-1, 2:])
    corner_u = 0.5 * (u_ext[:, :-1, 1:-1] + u_ext[:, 1:, 1:-1])
    flux_uu = cen_u * cen_u
    flux_vu = corner_v * corner_u
    tend_u = -(flux_uu[:, :, 1:] - flux_uu[:, :, :-1] + flux_vu[:, 1:, :] - flux_vu[:, :-1, :] + p_ext[:, 1:-1, 2:] - p_ext[:, 1:-1, 1:-1]) / GRID_DX
    cen_v = 0.5 * (v_ext[:, :-1, 1:-1] + v_ext[:, 1:, 1:-1])
    side_u = 0.5 * (u_ext[:, 1:-1, :-1] + u_ext[:, 2:, :-1])
    side_v = 0.5 * (v_ext[:, 1:-1, :-1] + v_ext[:, 1:-1, 1:])
    flux_vv = cen_v * cen_v
    flux_uv = side_u * side_v
    tend_v = -(flux_vv[:, 1:, :] - flux_vv[:, :-1, :] + flux_uv[:, :, 1:] - flux_uv[:, :, :-1] + p_ext[:, 2:, 1:-1] - p_ext[:, 1:-1, 1:-1]) / GRID_DX
    return tend_u, tend_v


def baroclinic_predict(vel_u, vel_v, value_a11, salinity, layout, halo_fn):
    n_levels = vel_u.shape[0]
    mask_c = level_mask(layout["k_cell"], n_levels)
    mask_u = level_mask(layout["k_u"], n_levels)
    mask_v = level_mask(layout["k_v"], n_levels)
    vel_um = vel_u * mask_u
    vel_vm = vel_v * mask_v
    density = mask_c * (BETA_S * (salinity - S_REF) - ALPHA_T * (value_a11 - T_REF))
    pressure = GRAVITY * layout["dz_cell"] * (jnp.cumsum(density, axis=0) - 0.5 * density)
    cell_coef = interface_coef(layout["k_cell"], layout["dz_cell"], DIFF_KT, n_levels)
    temp_mix = column_solve(value_a11 * mask_c, cell_coef)
    salt_mix = column_solve(salinity * mask_c, cell_coef)
    edges = halo_fn(jnp.stack([vel_um, vel_vm, pressure, temp_mix, salt_mix]))
    tend_u, tend_v = momentum_tend(edges[0], edges[1], edges[2])
    u_star = column_solve(mask_u * (vel_um + TIME_STEP * tend_u), interface_coef(layout["k_u"], layout["dz_u"], VISC_KV, n_levels))
    v_star = column_solve(mask_v * (vel_vm + TIME_STEP * tend_v), interface_coef(layout["k_v"], layout["dz_v"], VISC_KV, n_levels))
    forcing = jnp.stack([jnp.sum(layout["dz_u"] * (u_star - vel_um), axis=0), jnp.sum(layout["dz_v"] * (v_star - vel_vm), axis=0)]) / TIME_STEP
    return u_star, v_star, forcing, edges[3:], (mask_c, mask_u, mask_v)


def barotropic(eta_start, trans_start, face_depth, face_wet, wet_cell, forcing, tide_force, halo_fn):
    n_sub = tide_force.shape[0]
    dt_sub = TIME_STEP / n_sub
    weight_norm = 6.0 / (n_sub * (n_sub + 1) * (n_sub + 2))

    def substep(step, carry):
        eta_now, trans_now, trans_avg = carry
        trans_ext = halo_fn(trans_now)
        divergence = (trans_now[0] - trans_ext[0, 1:-1, :-2] + trans_now[1] - trans_ext[1, :-2, 1:-1]) / GRID_DX
        eta_next = wet_cell * (eta_now - dt_sub * divergence)
        eta_ext = halo_fn(eta_next)
        slope = jnp.stack([eta_ext[1:-1, 2:] - eta_next, eta_ext[2:, 1:-1] - eta_next]) / GRID_DX
        tide_now = lax.dynamic_index_in_dim(tide_force, step, 0, keepdims=False)
        trans_next = face_wet * (trans_now + dt_sub * (face_depth * (tide_now[:, None, None] - GRAVITY * slope) + forcing))
        weight = weight_norm * ((step + 1) * (n_sub - step)).astype(jnp.float32)
        return eta_next, trans_next, trans_avg + weight * trans_next

    return lax.fori_loop(0, n_sub, substep, (eta_start, trans_start, jnp.zeros_like(trans_start)))


def correct_velocity(star, dz_face, depth_face, mean_trans, mask):
    safe = jnp.where(depth_face > 0, depth_face, 1.0)
    return mask * (star + ((mean_trans - jnp.sum(dz_face * star, axis=0)) / safe)[None])


def advect_tracers(tracer_ext, flow_ext, mask_c):
    flux_x = flow_ext[0, :, 1:-1, :-1] * (0.5 * (tracer_ext[..., 1:-1, :-1] + tracer_ext[..., 1:-1, 1:]))
    flux_y = flow_ext[1, :, :-1, 1:-1] * (0.5 * (tracer_ext[..., :-1, 1:-1] + tracer_ext[..., 1:, 1:-1]))
    divergence = (flux_x[..., 1:] - flux_x[..., :-1] + flux_y[..., 1:, :] - flux_y[..., :-1, :]) / GRID_DX
    return mask_c * (tracer_ext[..., 1:-1, 1:-1] - TIME_STEP * divergence)


def baroclinic_finish(u_star, v_star, trans_avg, face_depth, layout, tracer_ext, masks, halo_fn):
    mask_c, mask_u, mask_v = masks
    vel_uc = correct_velocity(u_star, layout["dz_u"], face_depth[0], trans_avg[0], mask_u)
    vel_vc = correct_velocity(v_star, layout["dz_v"], face_depth[1], trans_avg[1], mask_v)
    flows = halo_fn(jnp.stack([vel_uc, vel_vc]))
    tracers = advect_tracers(tracer_ext, flows, mask_c)
    return vel_uc, vel_vc, tracers[0], tracers[1]


def ocean_step(vel_u, vel_v, value_a11, salinity, sea_level, trans_u, trans_v, bathymetry, kmt_levels, tide_force, halo_fn):
    layout = geometry(halo_fn(kmt_levels), halo_fn(bathymetry))
    u_star, v_star, forcing, tracer_ext, masks = baroclinic_predict(vel_u, vel_v, value_a11, salinity, layout, halo_fn)
    face_depth, face_wet, wet_cell = surface_fields(layout)
    eta_new, trans_new, trans_avg = barotropic(wet_cell * sea_level, face_wet * jnp.stack([trans_u, trans_v]), face_depth, face_wet, wet_cell, forcing, tide_force, halo_fn)
    vel_uc, vel_vc, temp_new, salt_new = baroclinic_finish(u_star, v_star, trans_avg, face_depth, layout, tracer_ext, masks, halo_fn)
    return eta_new, trans_new[0], trans_new[1], vel_uc, vel_vc, temp_new, salt_new


def solution(mesh):
    n_cols = mesh.shape["col"]
    n_rows = mesh.shape["row"]
    east_perm = [(member, (member - 1) % n_cols) for member in range(n_cols)]
    west_perm = [(member, (member + 1) % n_cols) for member in range(n_cols)]
    north_perm = [(member, member - 1) for member in range(1, n_rows)]
    south_perm = [(member, member + 1) for member in range(n_rows - 1)]

    def halo_swap(field):
        from_east = lax.ppermute(field[..., :1], "col", east_perm)
        from_west = lax.ppermute(field[..., -1:], "col", west_perm)
        wide = jnp.concatenate([from_west, field, from_east], axis=-1)
        from_north = lax.ppermute(wide[..., :1, :], "row", north_perm)
        from_south = lax.ppermute(wide[..., -1:, :], "row", south_perm)
        return jnp.concatenate([from_south, wide, from_north], axis=-2)

    def local_step(vel_u, vel_v, value_a11, salinity, sea_level, trans_u, trans_v, bathymetry, kmt_levels, tide_force):
        return ocean_step(vel_u, vel_v, value_a11, salinity, sea_level, trans_u, trans_v, bathymetry, kmt_levels, tide_force, halo_swap)

    spec_cube = P(None, "row", "col")
    spec_plane = P("row", "col")
    return jax.shard_map(local_step, mesh=mesh, in_specs=(spec_cube, spec_cube, spec_cube, spec_cube, spec_plane, spec_plane, spec_plane, spec_plane, spec_plane, P(None, None)), out_specs=(spec_plane, spec_plane, spec_plane, spec_cube, spec_cube, spec_cube, spec_cube), check_vma=False)
```

profile of v0, /device:TPU:0, one launch (start us, length us, event | category | flops | bytes accessed | tf_op | source)
XLA Modules:
  0.0 1193.9 jit_solution(18124601497335154399)
XLA Ops:
  8.0 10.4 fusion.61
  34.8 6.0 compare_select_fusion.2
  40.8 10.7 fusion.99
  57.6 44.4 %while.156 = (s32[]{:T(128)}, f32[128,512]{1,0:T(8,128)S(1)}, f32[128,512]{1,0:T(8,128)S(1)}, f32[20,128,512]{2,1,0:T(8,128)}, f32[20,128,512]{2,1,0:T(8,128)}, ...) while((s32[]{:T(128)}, f32[128,512]{1,0:T(8,128)S(1)}, ...), condition=%wide.region_6.7_spmd.clone, body=%wide.region_5.6_spmd.clone.sunk | while | flops 524291 | bytes 2622071 | solution.py:44
  105.0 39.2 %while.157 = (s32[]{:T(128)}, f32[128,512]{1,0:T(8,128)S(1)}, f32[20,128,512]{2,1,0:T(8,128)}, f32[20,128,512]{2,1,0:T(8,128)}, f32[20,128,512]{2,1,0:T(8,128)}, /*index=5*/s32[]{:T(128)}, s32[]{:T(128)}, s32[]{:T(128)}) while((s32[]{:T(128)}, f32[128,512]{1,0:T(8,128)S(1)}, f32[20,128,512]{2,1,0:T(8,128)}, ...), condition=%wide.region_8.9_spmd.clone, body=%wide.region_7.8_spmd.clone.sunk | while | flops 196612 | bytes 1310831 | solution.py:51
  150.3 44.2 %while.154 = (s32[]{:T(128)}, f32[128,512]{1,0:T(8,128)S(1)}, f32[128,512]{1,0:T(8,128)S(1)}, f32[20,128,512]{2,1,0:T(8,128)}, f32[20,128,512]{2,1,0:T(8,128)}, ...) while((s32[]{:T(128)}, f32[128,512]{1,0:T(8,128)S(1)}, ...), condition=%wide.region_2.3_spmd.clone, body=%wide.region_1.2_spmd.clone.sunk | while | flops 524291 | bytes 2622071 | solution.py:44
  197.6 39.3 %while.155 = (s32[]{:T(128)}, f32[128,512]{1,0:T(8,128)S(1)}, f32[20,128,512]{2,1,0:T(8,128)}, f32[20,128,512]{2,1,0:T(8,128)}, f32[20,128,512]{2,1,0:T(8,128)}, /*index=5*/s32[]{:T(128)}, s32[]{:T(128)}, s32[]{:T(128)}) while((s32[]{:T(128)}, f32[128,512]{1,0:T(8,128)S(1)}, f32[20,128,512]{2,1,0:T(8,128)}, ...), condition=%wide.region_4.5_spmd.clone, body=%wide.region_3.4_spmd.clone.sunk | while | flops 196612 | bytes 1310831 | solution.py:51
  236.9 5.9 bitcast_dynamic-update-slice_fusion.14
  246.3 11.1 bitcast_dynamic-update-slice_fusion.12
  263.9 11.5 fusion.97
  286.9 10.5 fusion.98
  297.4 10.7 fusion.100
  330.4 15.3 %maximum_bitcast_fusion.1 = (f32[20,130,514]{2,1,0:T(8,128)S(1)}, f32[20,130,514]{2,1,0:T(8,128)}, f32[20,130,514]{2,1,0:T(8,128)}) fusion(f32[5,20,1,514]{3,2,1,0:T(1,128)S(1)} %collective-permute-done.17, f32[5,20,1,514]{3,2,1,0:T(1,128)S(1)} %collective-permute-done.16, f32[5,20,128,1]{3,2,1,0:T(8,128)S(1)} %copy-done.1, ...), kind=kLoop, calls=%fused_computation.99 | loop fusion | flops 16036800 | bytes 42764800 | tf_op jit(solution)/shard_map/squeeze | solution.py:99
  345.7 13.7 %fusion.42 = (f32[20,128,513]{2,1,0:T(8,128)}, f32[20,128,513]{2,1,0:T(8,128)}) fusion(f32[20,130,514]{2,1,0:T(8,128)S(1)} %get-tuple-element.1206, f32[20,130,514]{2,1,0:T(8,128)} %get-tuple-element.1207), kind=kLoop, calls=%fused_computation.111 | loop fusion | flops 10506240 | bytes 36771840 | tf_op jit(solution)/shard_map/mul | solution.py:74
  359.4 17.6 %fusion.48 = (f32[20,129,512]{2,1,0:T(8,128)}, f32[20,129,512]{2,1,0:T(8,128)}) fusion(f32[20,130,514]{2,1,0:T(8,128)S(1)} %get-tuple-element.1206, f32[20,130,514]{2,1,0:T(8,128)} %get-tuple-element.1207), kind=kLoop, calls=%fused_computation.123 | loop fusion | flops 10567680 | bytes 36986880 | tf_op jit(solution)/shard_map/mul | solution.py:75
  376.9 31.2 %fusion.59 = (f32[20,128,512]{2,1,0:T(8,128)}, f32[20,128,512]{2,1,0:T(8,128)}) fusion(f32[20,130,514]{2,1,0:T(8,128)} %get-tuple-element.1208, f32[20,129,512]{2,1,0:T(8,128)} %get-tuple-element.1221, f32[20,128,513]{2,1,0:T(8,128)} %get-tuple-element.1219, f32[20,128,512]{2,1,0:T(8,128)} %param.28, s32[128,512]{1,0:T(8,128)S(1)} %get-tuple-element.1186, ...), kind=kLoop, calls=%fused_computation.142 | loop fusion | flops 28835840 | bytes 79167488 | tf_op jit(solution)/shard_map/mul | solution.py:100
  414.1 44.2 %while.158 = (s32[]{:T(128)}, f32[128,512]{1,0:T(8,128)S(1)}, f32[128,512]{1,0:T(8,128)S(1)}, f32[20,128,512]{2,1,0:T(8,128)}, f32[20,128,512]{2,1,0:T(8,128)}, ...) while((s32[]{:T(128)}, f32[128,512]{1,0:T(8,128)S(1)}, ...), condition=%wide.region_10.11_spmd.clone, body=%wide.region_9.10_spmd.clone.sunk | while | flops 524291 | bytes 2622071 | solution.py:44
  461.3 39.3 %while.159 = (s32[]{:T(128)}, f32[128,512]{1,0:T(8,128)S(1)}, f32[20,128,512]{2,1,0:T(8,128)}, f32[20,128,512]{2,1,0:T(8,128)}, f32[20,128,512]{2,1,0:T(8,128)}, /*index=5*/s32[]{:T(128)}, s32[]{:T(128)}, s32[]{:T(128)}) while((s32[]{:T(128)}, f32[128,512]{1,0:T(8,128)S(1)}, f32[20,128,512]{2,1,0:T(8,128)}, ...), condition=%wide.region_12.13_spmd.clone, body=%wide.region_11.12_spmd.clone.sunk | while | flops 196612 | bytes 1310831 | solution.py:51
  500.6 6.3 multiply_reduce_fusion.1
  513.0 44.2 %while.160 = (s32[]{:T(128)}, f32[128,512]{1,0:T(8,128)S(1)}, f32[128,512]{1,0:T(8,128)S(1)}, f32[20,128,512]{2,1,0:T(8,128)}, f32[20,128,512]{2,1,0:T(8,128)}, ...) while((s32[]{:T(128)}, f32[128,512]{1,0:T(8,128)S(1)}, ...), condition=%wide.region_15.16_spmd.clone, body=%wide.region_14.15_spmd.clone.sunk | while | flops 524291 | bytes 2622071 | solution.py:44
  560.2 39.1 %while.161 = (s32[]{:T(128)}, f32[128,512]{1,0:T(8,128)S(1)}, f32[20,128,512]{2,1,0:T(8,128)}, f32[20,128,512]{2,1,0:T(8,128)}, f32[20,128,512]{2,1,0:T(8,128)}, /*index=5*/s32[]{:T(128)}, s32[]{:T(128)}, s32[]{:T(128)}) while((s32[]{:T(128)}, f32[128,512]{1,0:T(8,128)S(1)}, f32[20,128,512]{2,1,0:T(8,128)}, ...), condition=%wide.region_17.18_spmd.clone, body=%wide.region_16.17_spmd.clone.sunk | while | flops 196612 | bytes 1310831 | solution.py:51
  599.4 6.3 multiply_reduce_fusion
  605.8 492.4 %while.162 = (s32[]{:T(128)}, f32[128,512]{1,0:T(8,128)S(1)}, f32[2,128,512]{2,1,0:T(8,128)S(1)}, f32[2,128,512]{2,1,0:T(8,128)S(1)}, f32[128,512]{1,0:T(8,128)}...) while((s32[]{:T(128)}, f32[128,512]{1,0:T(8,128)S(1)}, ...), condition=%wide.region_20.21_spmd.clone, body=%wide.region_19.20_spmd.clone.sunk | while | flops 2362387 | bytes 7925323 | solution.py:123
  612.6 6.2 collective-permute-start.2
  637.8 5.3 collective-permute-start.2
  661.4 6.0 collective-permute-start.2
  733.1 6.6 collective-permute-start.2
  757.9 6.3 collective-permute-start.2
  782.9 6.3 collective-permute-start.2
  807.4 6.3 collective-permute-start.2
  832.5 6.3 collective-permute-start.2
  857.0 6.3 collective-permute-start.2
  882.1 6.3 collective-permute-start.2
  906.6 6.3 collective-permute-start.2
  931.6 6.3 collective-permute-start.2
  956.1 6.3 collective-permute-start.2
  981.2 6.3 collective-permute-start.2
  1005.7 6.3 collective-permute-start.2
  1030.8 6.3 collective-permute-start.2
  1055.3 6.3 collective-permute-start.2
  1080.3 6.3 collective-permute-start.2
  1100.3 5.7 add_select_fusion
  1120.4 6.3 fusion.37
  1130.6 6.8 collective-permute-start.20
  1137.5 16.1 %fusion.29 = f32[2,20,128,513]{3,2,1,0:T(8,128)} fusion(f32[5,20,128,1]{3,2,1,0:T(8,128)} %copy.21, f32[5,20,128,512]{3,2,1,0:T(8,128)} %constant_dynamic-update-slice_fusion, f32[5,20,128,1]{3,2,1,0:T(8,128)} %copy.20, f32[20,128,513]{2,1,0:T(8,128)} %fusion.37), kind=kLoop, calls=%fused_computation.77 | loop fusion | flops 10506240 | bytes 42076160 | tf_op jit(solution)/shard_map/mul | solution.py:132
  1156.8 10.7 fusion.31
  1167.5 15.8 %fusion.34 = f32[2,20,128,512]{3,2,1,0:T(8,128)} fusion(f32[2,20,129,512]{3,2,1,0:T(8,128)S(1)} %fusion.31, f32[2,20,128,513]{3,2,1,0:T(8,128)} %fusion.29, f32[1,20,128,512]{3,2,1,0:T(8,128)S(1)} %bitcast.278, f32[1,20,128,512]{3,2,1,0:T(8,128)} %bitcast.279, f32[20,128,512]{2,1,0:T(8,128)} %fusion.60), kind=kLoop, calls=%fused_computation.90 | loop fusion | flops 18350080 | bytes 68157440 | tf_op jit(solution)/shard_map/mul | solution.py:135
  1183.4 10.3 slice_bitcast_fusion
  (746 shorter events, 839.7 us)
Async XLA Ops:
  1.6 19.9 %collective-permute-start.6 = (s32[128,1]{1,0:T(8,128)S(1)}, s32[128,1]{1,0:T(8,128)S(1)}, u32[]{:S(2)}, u32[]{:S(2)}) collective-permute-start(s32[128,1]{1,0:T(8,128)S(1)} %get-tuple-element.1249), channel_id=1, source_target_pairs={{0,8},{8,0},{1,9},{9,1},{2,10},{10,2},{3,11},{11,3},{4,12},{12,4},... | collective-permute-start | bytes 1544 | tf_op jit(solution)/shard_map/ppermute | solution.py:165
  4.9 16.5 %collective-permute-start.7 = (s32[128,1]{1,0:T(8,128)S(1)}, s32[128,1]{1,0:T(8,128)S(1)}, u32[]{:S(2)}, u32[]{:S(2)}) collective-permute-start(s32[128,1]{1,0:T(8,128)S(1)} %get-tuple-element.1248), channel_id=1, source_target_pairs={{0,8},{8,0},{1,9},{9,1},{2,10},{10,2},{3,11},{11,3},{4,12},{12,4},... | collective-permute-start | bytes 1544 | tf_op jit(solution)/shard_map/ppermute | solution.py:166
  5.9 19.9 %collective-permute-start.10 = (f32[128,1]{1,0:T(8,128)S(1)}, f32[128,1]{1,0:T(8,128)S(1)}, u32[]{:S(2)}, u32[]{:S(2)}) collective-permute-start(f32[128,1]{1,0:T(8,128)S(1)} %get-tuple-element.1251), channel_id=1, source_target_pairs={{0,8},{8,0},{1,9},{9,1},{2,10},{10,2},{3,11},{11,3},{4,12},{12,4},... | collective-permute-start | bytes 1544 | tf_op jit(solution)/shard_map/ppermute | solution.py:165
  7.9 17.9 %collective-permute-start.9 = (f32[128,1]{1,0:T(8,128)S(1)}, f32[128,1]{1,0:T(8,128)S(1)}, u32[]{:S(2)}, u32[]{:S(2)}) collective-permute-start(f32[128,1]{1,0:T(8,128)S(1)} %get-tuple-element.1250), channel_id=1, source_target_pairs={{0,8},{8,0},{1,9},{9,1},{2,10},{10,2},{3,11},{11,3},{4,12},{12,4},... | collective-permute-start | bytes 1544 | tf_op jit(solution)/shard_map/ppermute | solution.py:166
  21.5 10.0 collective-permute-start.8
  22.8 8.7 collective-permute-start.13
  26.0 5.5 collective-permute-start.11
  280.0 30.8 %collective-permute-start.14 = (f32[5,20,128,1]{2,3,1,0:T(1,128)S(1)}, f32[5,20,128,1]{2,3,1,0:T(1,128)S(1)}, u32[]{:S(2)}, u32[]{:S(2)}) collective-permute-start(f32[5,20,128,1]{2,3,1,0:T(1,128)S(1)} %copy.18), channel_id=1, source_target_pairs={{0,8},{8,0},{1,9},{9,1},{2,10},{10,2},{3,11},{11,3},{4,12},{12,4},... | collective-permute-start | bytes 153608 | tf_op jit(solution)/shard_map/ppermute | solution.py:166
  286.4 28.5 %collective-permute-start.15 = (f32[5,20,128,1]{2,3,1,0:T(1,128)S(1)}, f32[5,20,128,1]{2,3,1,0:T(1,128)S(1)}, u32[]{:S(2)}, u32[]{:S(2)}) collective-permute-start(f32[5,20,128,1]{2,3,1,0:T(1,128)S(1)} %copy.19), channel_id=1, source_target_pairs={{0,8},{8,0},{1,9},{9,1},{2,10},{10,2},{3,11},{11,3},{4,12},{12,4},... | collective-permute-start | bytes 153608 | tf_op jit(solution)/shard_map/ppermute | solution.py:165
  322.9 5.3 collective-permute-start.16
  612.6 7.0 collective-permute-start.2
  632.1 5.6 collective-permute-start.1
  637.8 6.1 collective-permute-start.2
  661.4 6.8 collective-permute-start.2
  670.7 5.2 collective-permute-start.4
  680.9 6.3 collective-permute-start.1
  693.9 5.3 collective-permute-start.4
  704.2 5.3 collective-permute-start.1
  709.6 5.5 collective-permute-start.2
  727.3 5.7 collective-permute-start.1
  733.1 7.4 collective-permute-start.2
  752.7 5.1 collective-permute-start.1
  757.9 7.1 collective-permute-start.2
  777.2 5.6 collective-permute-start.1
  782.9 7.1 collective-permute-start.2
  802.3 5.1 collective-permute-start.1
  807.4 7.1 collective-permute-start.2
  826.8 5.6 collective-permute-start.1
  832.5 7.1 collective-permute-start.2
  851.8 5.1 collective-permute-start.1
  857.0 7.1 collective-permute-start.2
  876.3 5.6 collective-permute-start.1
  882.1 7.1 collective-permute-start.2
  906.6 7.1 collective-permute-start.2
  925.9 5.6 collective-permute-start.1
  931.6 7.1 collective-permute-start.2
  956.1 7.1 collective-permute-start.2
  975.5 5.6 collective-permute-start.1
  981.2 7.1 collective-permute-start.2
  1005.7 7.1 collective-permute-start.2
  1025.0 5.6 collective-permute-start.1
  1030.8 7.1 collective-permute-start.2
  1055.3 7.1 collective-permute-start.2
  1074.6 5.6 collective-permute-start.1
  1080.3 7.1 collective-permute-start.2
  1114.2 5.4 collective-permute-start.18
  1118.0 8.7 collective-permute-start.19
  1130.6 22.9 %collective-permute-start.20 = (f32[2,20,1,514]{3,2,1,0:T(1,128)S(1)}, f32[2,20,1,514]{3,2,1,0:T(1,128)S(1)}, u32[]{:S(2)}, u32[]{:S(2)}) collective-permute-start(f32[2,20,1,514]{3,2,1,0:T(1,128)S(1)} %pad_maximum_fusion.35), channel_id=1, source_target_pairs={{0,1},{1,2},{2,3},{3,4},{4,5},{5,6},{6,7},{8,9},{9,10},{10,11},{11... | collective-permute-start | bytes 246728 | tf_op jit(solution)/shard_map/ppermute | solution.py:169
  (142 other events, 2152.6 us)
where the time goes:
time: 1210 us; the launch traced here: 1190 us
  other arithmetic  610 us (50%)
  starting transfers between devices  259 us (21%)
  waiting for transfers between devices  209 us (17%)
  local copies, waits for them, and re-layouts  113 us (9%)
    dynamic_update_slice x160, other arithmetic, column_solve(): _, (gains, parts) = lax.scan(forward, start, (lower, diag, upper, source))  334 us
    ppermute x24, starting transfers between devices, halo_swap(): from_south = lax.ppermute(wide[..., -1:, :], 'row', south_perm)  138 us
    ppermute x44, waiting for transfers between devices, halo_swap(): from_east = lax.ppermute(field[..., :1], 'col', east_perm)  105 us
    ppermute x44, waiting for transfers between devices, halo_swap(): from_west = lax.ppermute(field[..., -1:], 'col', west_perm)  63.3 us
    ppermute x44, starting transfers between devices, halo_swap(): from_east = lax.ppermute(field[..., :1], 'col', east_perm)  49.6 us
    ppermute x44, starting transfers between devices, halo_swap(): from_west = lax.ppermute(field[..., -1:], 'col', west_perm)  41.8 us
    another operation x12, local copies, waits for them, and re-layouts  36.2 us
    concatenate x3, other arithmetic, column_solve(): lower = jnp.concatenate([edge, couple], axis=0)  31.9 us
  transfers between devices with their start and end apart: 135, of which 122 were waited for; matrix products, arithmetic and copies ran while one was open for 7% of the time, Pallas kernels for 0%

commit v1 on v0

v1 whole, which is shorter than its diff:
```python
import functools

import jax
import jax.numpy as jnp
from jax import lax
from jax.experimental import pallas as pl
from jax.experimental.pallas import tpu as pltpu
from jax.sharding import PartitionSpec as P

TIME_STEP = 4.0
ALPHA_T = 0.02
BETA_S = 0.015
VISC_KV = 0.001
DIFF_KT = 0.0005

NL = 20
NSUB = 20
NR, NC = 128, 512
HR = 24
ER, EC = NR + 2 * HR, NC + 128
NCH = 4
CH = NR // NCH
DTB = TIME_STEP / NSUB
F32 = jnp.float32
ZERO = 0.0
BODY = slice(0, NC)
LEFT = slice(0, 128)
RIGHT = slice(NC - 128, NC)
GHOST = slice(NC, EC)
KMT, DZ, ETA, TU, TV, FX, FY, SV, SU = range(9)
WIDE = 42
MESH = pl.DeviceIdType.MESH


def rows(r, off=0):
    start = 8 * r + off
    if isinstance(start, int):
        return pl.ds(start, 8)
    return pl.ds(pl.multiple_of(start, 8), 8)


def iota(shape, axis):
    return lax.broadcasted_iota(jnp.int32, shape, axis)


def east(x):
    return pltpu.roll(x, x.shape[1] - 1, 1)


def west(x):
    return pltpu.roll(x, 1, 1)


def north(here, above):
    return pltpu.roll(jnp.where(iota(here.shape, 0) == 0, above, here), 7, 0)


def south(here, below):
    return pltpu.roll(jnp.where(iota(here.shape, 0) == 7, below, here), 1, 0)


def lane_of(slot, k):
    return 2 * k + 40 * slot


def unpack(ghost, slot, k):
    shift = (128 - lane_of(slot, k)) % 128
    return pltpu.roll(ghost, shift, 1) if shift else ghost


def pack(tiles):
    lane = iota((8, 128), 1)
    acc = None
    first = None
    for slot, k, low, high in tiles:
        both = jnp.where(lane == 127, high, low)
        at = lane_of(slot, k)
        moved = pltpu.roll(both, at, 1) if at else both
        if acc is None:
            acc = moved
            if at == 0:
                first = moved
        else:
            acc = jnp.where(lane >= at - 1, moved, acc)
    if first is not None:
        acc = jnp.where(lane == 127, first, acc)
    return acc


def pack_wide(planes):
    lane = iota((8, 128), 1)
    acc = None
    for q, x in enumerate(planes):
        edge = jnp.where(lane < 64, x[:, LEFT], x[:, RIGHT])
        if acc is None:
            acc = edge
        else:
            acc = jnp.where(lane >= WIDE * q - WIDE // 2, pltpu.roll(edge, WIDE * q, 1), acc)
    if len(planes) == 1:
        return acc
    first = jnp.where(lane < 64, planes[0][:, LEFT], planes[0][:, RIGHT])
    return jnp.where(lane >= 128 - WIDE // 2, first, acc)


def unpack_wide(tile, q):
    lane = iota((8, 128), 1)
    moved = pltpu.roll(tile, 128 - WIDE * q, 1) if q else tile
    return jnp.where((lane < WIDE // 2) | (lane >= 128 - WIDE // 2), moved, ZERO)


def solve(refs, masked, count, coef, gains, at):
    low = gain = None
    parts = [None] * len(refs)
    for k in range(NL):
        up = jnp.where(count > k + 1.0, coef, ZERO) if k < NL - 1 else None
        if k == 0:
            pivot = 1.0 + up
        elif k < NL - 1:
            pivot = (1.0 + up) + low * (1.0 - gain)
        else:
            pivot = 1.0 + low * (1.0 - gain)
        inv = 1.0 / pivot
        for i, ref in enumerate(refs):
            src = ref[k, at, :]
            if not masked:
                src = jnp.where(count > k, src, ZERO)
            parts[i] = src * inv if k == 0 else (src + low * parts[i]) * inv
            if k < NL - 1:
                ref[k, at, :] = parts[i]
        if k < NL - 1:
            gain = up * inv
            gains[k] = gain
        low = up
    for i, ref in enumerate(refs):
        ref[NL - 1, at, :] = parts[i]
    for k in range(NL - 2, -1, -1):
        gain = gains[k]
        for i, ref in enumerate(refs):
            parts[i] = ref[k, at, :] + gain * parts[i]
            ref[k, at, :] = parts[i]


def predict_kernel(
    u_h, v_h, t_h, s_h, eta_h, tu_h, tv_h, dep_h, kmt_h,
    su_o, sv_o, tm_o, sm_o, ext_o, gts_o, gu_o, grts_o, grtn_o, grv_o,
    ub, vb, pb, tb, sb, su, sv, ext, ktmp, htmp, pa, pb_, pc, ga, gb, gc, ug, vg, pg, dup, sp, gx, prn, prs, grs, grn, sts, trn, trs, sug, vrn, fp, gains, gains2,
    load_sem, small_sem, out_sem, outs_sem, send_sem, recv_sem,
):
    col = lax.axis_index("col")
    row = lax.axis_index("row")
    n_row = 8
    side = 1 - col
    up_row = lax.rem(row + 1, n_row)
    down_row = lax.rem(row + n_row - 1, n_row)
    to_x = {"col": side, "row": row}
    to_n = {"col": col, "row": up_row}
    to_s = {"col": col, "row": down_row}
    to_dn = {"col": side, "row": up_row}
    to_ds = {"col": side, "row": down_row}

    barrier = pltpu.get_barrier_semaphore()
    for dev in (to_x, to_n, to_s, to_dn, to_ds):
        pl.semaphore_signal(barrier, inc=1, device_id=dev, device_id_type=MESH)

    small = [
        pltpu.make_async_copy(kmt_h, ktmp, small_sem.at[0]),
        pltpu.make_async_copy(dep_h, htmp, small_sem.at[1]),
        pltpu.make_async_copy(eta_h, ext.at[2, pl.ds(HR, NR), pl.ds(0, NC)], small_sem.at[2]),
        pltpu.make_async_copy(tu_h, ext.at[3, pl.ds(HR, NR), pl.ds(0, NC)], small_sem.at[3]),
        pltpu.make_async_copy(tv_h, ext.at[4, pl.ds(HR, NR), pl.ds(0, NC)], small_sem.at[4]),
    ]
    for c in small:
        c.start()

    def load(i, c):
        src = (t_h, s_h, u_h, v_h)[i]
        dst = (tb, sb, ub, vb)[i]
        at = pl.ds(pl.multiple_of(c * CH, CH), CH)
        to = pl.ds(pl.multiple_of(c * CH + (8 if i >= 2 else 0), 8), CH)
        return pltpu.make_async_copy(src.at[:, at, :], dst.at[:, to, :], load_sem.at[i, c])

    def start_loads(pair):
        def body(c, _):
            for i in pair:
                load(i, c).start()
            return 0

        lax.fori_loop(0, NCH, body, 0)

    start_loads((0, 1))
    start_loads((2, 3))

    def send(src, dst, idx, dev):
        c = pltpu.make_async_remote_copy(
            src_ref=src, dst_ref=dst, send_sem=send_sem.at[idx], recv_sem=recv_sem.at[idx], device_id=dev, device_id_type=MESH
        )
        c.start()
        return c

    for c in small:
        c.wait()
    def stage(r, _):
        kf = ktmp[rows(r), :].astype(F32)
        dz = htmp[rows(r), :] / jnp.maximum(kf, 1.0)
        ext[KMT, rows(r, HR), BODY] = kf
        ext[DZ, rows(r, HR), BODY] = dz
        eta, tu, tv = (ext[f, rows(r, HR), BODY] for f in (ETA, TU, TV))
        pa[rows(r), :] = pack_wide((kf, dz, eta))
        pb_[rows(r), :] = pack_wide((tu, tv))
        return 0

    lax.fori_loop(0, NR // 8, stage, 0)
    pl.semaphore_wait(barrier, 5)

    def send_ext(lo, n, tile, ghost, base):
        at = pl.ds(lo, n)
        low, high, mid = pl.ds(0, HR), pl.ds(HR + NR, HR), pl.ds(HR, NR)
        body = pl.ds(0, NC)
        return [
            send(tile, ghost.at[mid, :], base, to_x),
            send(ext.at[at, pl.ds(NR, HR), body], ext.at[at, low, body], base + 1, to_n),
            send(ext.at[at, pl.ds(HR, HR), body], ext.at[at, high, body], base + 2, to_s),
            send(tile.at[pl.ds(NR - HR, HR), :], ghost.at[low, :], base + 3, to_dn),
            send(tile.at[low, :], ghost.at[high, :], base + 4, to_ds),
        ]

    def receive_ext(copies, ghost, fields):
        for c in copies:
            c.wait()

        def body(t, _):
            g = ghost[rows(t), :]
            for q, f in enumerate(fields):
                ext[f, rows(t), GHOST] = unpack_wide(g, q)
            return 0

        lax.fori_loop(0, ER // 8, body, 0)

    first = send_ext(KMT, 3, pa, ga, 0)
    later = send_ext(TU, 2, pb_, gb, 5)

    def pressure(r, _):
        kc = ext[KMT, rows(r, HR), BODY]
        dz = ext[DZ, rows(r, HR), BODY]
        total = jnp.zeros((8, NC), F32)
        for k in range(NL):
            dens = BETA_S * (sb[k, rows(r), :] - 1.0) - ALPHA_T * (tb[k, rows(r), :] - 1.0)
            dens = jnp.where(kc > k, dens, ZERO)
            total = total + dens
            pb[k, rows(r, 8), :] = dz * (total - 0.5 * dens)
        return 0

    def pressure_chunk(c, _):
        load(0, c).wait()
        load(1, c).wait()
        lax.fori_loop(c * (CH // 8), (c + 1) * (CH // 8), pressure, 0)
        return 0

    lax.fori_loop(0, NCH, pressure_chunk, 0)

    receive_ext(first, ga, (KMT, DZ, ETA))
    has_south = (row > 0).astype(F32)
    has_north = (row < n_row - 1).astype(F32)
    ext[KMT, 0:HR, :] = ext[KMT, 0:HR, :] * has_south
    ext[KMT, HR + NR :, :] = ext[KMT, HR + NR :, :] * has_north

    def count_u(r):
        kc = ext[KMT, rows(r, HR), :]
        return jnp.minimum(kc, east(kc))[:, BODY]

    def count_v(r):
        kc = ext[KMT, rows(r, HR), BODY]
        return jnp.minimum(kc, north(kc, ext[KMT, rows(r, HR + 8), BODY]))

    def mask_pack(r, _):
        counts = (count_u(r), count_v(r))
        tiles = []
        for slot, ref in enumerate((ub, vb, pb)):
            for k in range(NL):
                x = ref[k, rows(r, 8), :]
                if slot < 2:
                    x = jnp.where(counts[slot] > k, x, ZERO)
                    ref[k, rows(r, 8), :] = x
                tiles.append((slot, k, x[:, LEFT], x[:, RIGHT]))
        sp[rows(r), :] = pack(tiles)
        return 0

    def mask_chunk(c, _):
        load(2, c).wait()
        load(3, c).wait()
        lax.fori_loop(c * (CH // 8), (c + 1) * (CH // 8), mask_pack, 0)
        return 0

    lax.fori_loop(0, NCH, mask_chunk, 0)

    def edge_row(dst, i, k, ref, at):
        dst[24 * i + k : 24 * i + k + 1, :] = ref[k, at : at + 1, :]

    def ghost_row(ref, k, at, src, i):
        ref[k, at : at + 1, :] = src[24 * i + k : 24 * i + k + 1, :]

    for k in range(NL):
        for i, ref in enumerate((ub, vb, pb)):
            edge_row(prs, i, k, ref, 8)
        for i, ref in enumerate((ub, vb)):
            edge_row(prn, i, k, ref, NR + 7)
    second = [
        send(sp, gx.at[pl.ds(8, NR), :], 10, to_x),
        send(prn, grs, 11, to_n),
        send(prs, grn, 12, to_s),
        send(sp.at[pl.ds(NR - 8, 8), :], gx.at[pl.ds(0, 8), :], 13, to_dn),
        send(sp.at[pl.ds(0, 8), :], gx.at[pl.ds(NR + 8, 8), :], 14, to_ds),
    ]

    def out_copy(i, c):
        src = (tb, sb, su, sv)[i]
        dst = (tm_o, sm_o, su_o, sv_o)[i]
        at = pl.ds(pl.multiple_of(c * CH, CH), CH)
        return pltpu.make_async_copy(src.at[:, at, :], dst.at[:, at, :], out_sem.at[i, c])

    def mix(r, _):
        kc = ext[KMT, rows(r, HR), BODY]
        dz = ext[DZ, rows(r, HR), BODY]
        solve((tb, sb), False, kc, (TIME_STEP * DIFF_KT) / (dz * dz), gains, rows(r))
        tiles = []
        for slot, ref in enumerate((tb, sb)):
            for k in range(NL):
                tiles.append((slot, k, ref[k, rows(r), LEFT], ref[k, rows(r), RIGHT]))
        sts[rows(r), :] = pack(tiles)
        return 0

    def mix_chunk(c, _):
        lax.fori_loop(c * (CH // 8), (c + 1) * (CH // 8), mix, 0)
        out_copy(0, c).start()
        out_copy(1, c).start()
        return 0

    lax.fori_loop(0, NCH, mix_chunk, 0)
    for k in range(NL):
        for i, ref in enumerate((tb, sb)):
            edge_row(trs, i, k, ref, 0)
            edge_row(trn, i, k, ref, NR - 1)
    third = [send(sts, gts_o, 15, to_x), send(trn, grts_o, 16, to_n), send(trs, grtn_o, 17, to_s)]

    for c in second:
        c.wait()

    def spread(s, _):
        g = gx[rows(s), :]
        for k in range(NL):
            for slot, ref in enumerate((ug, vg, pg)):
                ref[k, rows(s), :] = unpack(g, slot, k)
        return 0

    lax.fori_loop(0, NR // 8 + 2, spread, 0)
    for k in range(NL):
        for i, ref in enumerate((ub, vb)):
            ghost_row(ref, k, 7, grs, i)
        for i, ref in enumerate((ub, vb, pb)):
            ghost_row(ref, k, NR + 8, grn, i)

    def corner(r, k):
        here, above = ub[k, rows(r, 8), :], ub[k, rows(r, 16), :]
        g_here, g_above = ug[k, rows(r, 8), :], ug[k, rows(r, 16), :]
        u_e = jnp.concatenate([here, g_here], 1)
        un_e = jnp.concatenate([north(here, above), north(g_here, g_above)], 1)
        v = vb[k, rows(r, 8), :]
        v_e = jnp.concatenate([v, vg[k, rows(r, 8), :]], 1)
        f_e = 0.25 * ((v_e + east(v_e)) * (u_e + un_e))
        return u_e, v, f_e

    for k in range(NL):
        fp[k] = corner(-1, k)[2]

    def tendency(r, _):
        for k in range(NL):
            u_e, v, f_e = corner(r, k)
            f = f_e[:, BODY]
            f_s = south(f, fp[k, :, BODY])
            fp[k] = f_e
            p = pb[k, rows(r, 8), :]
            p_e = east(jnp.concatenate([p, pg[k, rows(r, 8), :]], 1))[:, BODY]
            p_n = north(p, pb[k, rows(r, 16), :])
            du = 0.5 * (u_e + east(u_e))
            du = du * du
            dup[k] = du
            hi = 0.5 * (v + north(v, vb[k, rows(r, 16), :]))
            lo = 0.5 * (v + south(v, vb[k, rows(r), :]))
            su[k, rows(r), :] = (f_s - f) + ((p - p_e) - du[:, BODY])
            sv[k, rows(r), :] = (lo * lo - hi * hi) + ((p - p_n) - f)
        k_u, k_v = count_u(r), count_v(r)
        acc_u = acc_v = sum_u = sum_v = jnp.zeros((8, NC), F32)
        for k in range(NL):
            u, v = ub[k, rows(r, 8), :], vb[k, rows(r, 8), :]
            t_u = jnp.where(k_u > k, su[k, rows(r), :] + west(dup[k])[:, BODY], ZERO)
            t_v = jnp.where(k_v > k, sv[k, rows(r), :] + west(fp[k])[:, BODY], ZERO)
            su[k, rows(r), :] = u + TIME_STEP * t_u
            sv[k, rows(r), :] = v + TIME_STEP * t_v
            acc_u, acc_v = acc_u + t_u, acc_v + t_v
            sum_u, sum_v = sum_u + u, sum_v + v
        dz_u, dz_v = face_dz(r)
        f_x, f_y = dz_u * acc_u, dz_v * acc_v
        s_u = dz_u * (sum_u + TIME_STEP * acc_u)
        ext[FX, rows(r, HR), BODY] = f_x
        ext[FY, rows(r, HR), BODY] = f_y
        ext[SU, rows(r, HR), BODY] = s_u
        ext[SV, rows(r, HR), BODY] = dz_v * (sum_v + TIME_STEP * acc_v)
        pc[rows(r), :] = pack_wide((f_x, f_y, s_u))
        return 0

    def face_dz(r):
        dz_e = ext[DZ, rows(r, HR), :]
        dz = dz_e[:, BODY]
        dz_u = 0.5 * (dz + east(dz_e)[:, BODY])
        dz_v = 0.5 * (dz + north(dz, ext[DZ, rows(r, HR + 8), BODY]))
        return dz_u, dz_v

    lax.fori_loop(0, NR // 8, tendency, 0)
    fourth = send_ext(FX, 3, pc, gc, 18)
    receive_ext(later, gb, (TU, TV))
    out_ext0 = pltpu.make_async_copy(ext.at[pl.ds(0, 5)], ext_o.at[pl.ds(0, 5)], outs_sem.at[0])
    out_ext0.start()

    def momentum(r, _):
        dz_u, dz_v = face_dz(r)
        solve((su,), True, count_u(r), (TIME_STEP * VISC_KV) / (dz_u * dz_u), gains, rows(r))
        solve((sv,), True, count_v(r), (TIME_STEP * VISC_KV) / (dz_v * dz_v), gains2, rows(r))
        sug[rows(r), :] = pack([(0, k, su[k, rows(r), LEFT], su[k, rows(r), RIGHT]) for k in range(NL)])
        return 0

    def momentum_chunk(c, _):
        lax.fori_loop(c * (CH // 8), (c + 1) * (CH // 8), momentum, 0)
        out_copy(2, c).start()
        out_copy(3, c).start()
        return 0

    lax.fori_loop(0, NCH, momentum_chunk, 0)
    for k in range(NL):
        edge_row(vrn, 0, k, sv, NR - 1)
    fifth = [send(sug, gu_o, 23, to_x), send(vrn, grv_o, 24, to_n)]
    receive_ext(fourth, gc, (FX, FY, SU))
    out_ext1 = pltpu.make_async_copy(ext.at[pl.ds(5, 4)], ext_o.at[pl.ds(5, 4)], outs_sem.at[1])
    out_ext1.start()

    def drain(c, _):
        for i in range(4):
            out_copy(i, c).wait()
        return 0

    lax.fori_loop(0, NCH, drain, 0)
    for c in third:
        c.wait()
    for c in fifth:
        c.wait()
    out_ext0.wait()
    out_ext1.wait()


def finish_kernel(
    tide, su_h, sv_h, tm_h, sm_h, ext_h, gts_h, gu_h, grts_h, grtn_h, grv_h,
    eta_o, tu_o, tv_o, u_o, v_o, t_o, s_o,
    ub, vb, tb, sb, ext, cof, avg, gts, gu, grts, grtn, grv, fpt, fps, fxt, fxs, ug, tg, sg,
    load_sem, small_sem, out_sem, outs_sem,
):
    early = pltpu.make_async_copy(ext_h, ext, small_sem.at[0])
    early.start()
    small = [
        pltpu.make_async_copy(a, b, small_sem.at[i + 1])
        for i, (a, b) in enumerate(((gts_h, gts), (gu_h, gu), (grts_h, grts), (grtn_h, grtn), (grv_h, grv)))
    ]
    for c in small:
        c.start()
    big = [
        pltpu.make_async_copy(su_h, ub, load_sem.at[0]),
        pltpu.make_async_copy(sv_h, vb.at[:, pl.ds(8, NR), :], load_sem.at[1]),
        pltpu.make_async_copy(tm_h, tb.at[:, pl.ds(8, NR), :], load_sem.at[2]),
        pltpu.make_async_copy(sm_h, sb.at[:, pl.ds(8, NR), :], load_sem.at[3]),
    ]
    for c in big:
        c.start()
    early.wait()

    def faces(at, above):
        kc, kn = ext[KMT, at, :], ext[KMT, above, :]
        dz, dn = ext[DZ, at, :], ext[DZ, above, :]
        k_u = jnp.minimum(kc, east(kc))
        k_v = jnp.minimum(kc, north(kc, kn))
        return kc, k_u, k_v, k_u * (0.5 * (dz + east(dz))), k_v * (0.5 * (dz + north(dz, dn)))

    def prepare(t, _):
        at = rows(t)
        kc, k_u, k_v, h_u, h_v = faces(at, rows(jnp.minimum(t + 1, ER // 8 - 1)))
        cof[0, at, :] = (DTB * DTB) * h_u
        cof[1, at, :] = (DTB * DTB) * h_v
        for f in (FX, FY):
            ext[f, at, :] = (DTB * DTB) * ext[f, at, :]
        for f, count, scale in ((ETA, kc, 1.0), (TU, k_u, DTB), (TV, k_v, DTB)):
            ext[f, at, :] = jnp.where(count > ZERO, scale * ext[f, at, :], ZERO)
        for i in range(2):
            avg[i, at, :] = jnp.zeros((8, EC), F32)
        return 0

    lax.fori_loop(0, ER // 8, prepare, 0)

    norm = 6.0 / (NSUB * (NSUB + 1) * (NSUB + 2)) / DTB

    def subcycle(n, _, lo, hi):
        tide_x, tide_y = tide[n, 0], tide[n, 1]
        weight = norm * ((n + 1) * (NSUB - n)).astype(F32)
        v_prev = ext[TV, rows(max(lo - 1, 0)), :]
        eta_prev = None
        u_keep = v_keep = None
        for t in range(lo, hi + 1):
            if t < hi:
                at = rows(t)
                u, v = ext[TU, at, :], ext[TV, at, :]
                eta = ext[ETA, at, :] - ((u - west(u)) + (v - south(v, v_prev)))
                ext[ETA, at, :] = eta
            if t > lo:
                b = rows(t - 1)
                slope_x = east(eta_prev) - eta_prev
                slope_y = north(eta_prev, eta) - eta_prev
                u_new = u_keep + (cof[0, b, :] * (tide_x - slope_x) + ext[FX, b, :])
                v_new = v_keep + (cof[1, b, :] * (tide_y - slope_y) + ext[FY, b, :])
                ext[TU, b, :] = u_new
                ext[TV, b, :] = v_new
                if 2 <= t - 1 < 19:
                    avg[0, b, :] = avg[0, b, :] + weight * u_new
                    avg[1, b, :] = avg[1, b, :] + weight * v_new
            eta_prev, u_keep, v_keep, v_prev = eta, u, v, v
        return 0

    tiles = ER // 8
    lax.fori_loop(0, 4, functools.partial(subcycle, lo=0, hi=tiles), 0)
    lax.fori_loop(4, 12, functools.partial(subcycle, lo=1, hi=tiles - 1), 0)
    lax.fori_loop(12, NSUB, functools.partial(subcycle, lo=2, hi=tiles - 2), 0)

    def unscale(r, _):
        at = rows(r, HR)
        for f in (TU, TV):
            ext[f, at, :] = (1.0 / DTB) * ext[f, at, :]
        return 0

    lax.fori_loop(0, NR // 8, unscale, 0)
    planes = [
        pltpu.make_async_copy(ext.at[2 + i, pl.ds(HR, NR), pl.ds(0, NC)], o, outs_sem.at[i])
        for i, o in enumerate((eta_o, tu_o, tv_o))
    ]
    for c in planes:
        c.start()
    for c in small:
        c.wait()
    for c in big:
        c.wait()
    for k in range(NL):
        vb[k, 7:8, :] = grv[k : k + 1, :]
        for i, ref in enumerate((tb, sb)):
            ref[k, 7:8, :] = grts[24 * i + k : 24 * i + k + 1, :]
            ref[k, NR + 8 : NR + 9, :] = grtn[24 * i + k : 24 * i + k + 1, :]

    def strip(r):
        at, above = rows(r, HR), rows(r, HR + 8)
        kc, k_u, k_v, h_u, h_v = faces(at, above)
        d_u = (avg[0, at, :] - ext[SU, at, :]) / jnp.where(h_u > ZERO, h_u, 1.0)
        d_v = (avg[1, at, BODY] - ext[SV, at, BODY]) / jnp.where(h_v > ZERO, h_v, 1.0)[:, BODY]
        return kc[:, BODY], k_u, k_v[:, BODY], d_u, d_v

    def flux_y(r, k, k_v, d_v):
        vc = jnp.where(k_v > k, vb[k, rows(r, 8), :] + d_v, ZERO)
        out = [vc]
        for ref in (tb, sb):
            here = ref[k, rows(r, 8), :]
            out.append(here)
            out.append(vc * (here + north(here, ref[k, rows(r, 16), :])))
        return out

    _, _, k_v, _, d_v = strip(-1)
    for k in range(NL):
        _, _, a, _, b = flux_y(-1, k, k_v, d_v)
        fpt[k] = a
        fps[k] = b

    def spread(r, _):
        g_u, g_ts = gu[rows(r), :], gts[rows(r), :]
        for k in range(NL):
            ug[k, rows(r), :] = unpack(g_u, 0, k)
            tg[k, rows(r), :] = unpack(g_ts, 0, k)
            sg[k, rows(r), :] = unpack(g_ts, 1, k)
        return 0

    lax.fori_loop(0, NR // 8, spread, 0)

    def advect(r, _):
        kc, k_u, k_v, d_u, d_v = strip(r)
        for k in range(NL):
            vc, t, y_t, s, y_s = flux_y(r, k, k_v, d_v)
            vb[k, rows(r, 8), :] = vc
            uc = jnp.where(k_u > k, jnp.concatenate([ub[k, rows(r), :], ug[k, rows(r), :]], 1) + d_u, ZERO)
            ub[k, rows(r), :] = uc[:, BODY]
            for ref, ghost, prev, keep, x, y in ((tb, tg, fpt, fxt, t, y_t), (sb, sg, fps, fxs, s, y_s)):
                x_e = jnp.concatenate([x, ghost[k, rows(r), :]], 1)
                fx = uc * (x_e + east(x_e))
                keep[k] = fx
                ref[k, rows(r, 8), :] = x - (0.5 * TIME_STEP) * (fx[:, BODY] + (y - south(y, prev[k])))
                prev[k] = y
        for k in range(NL):
            for ref, keep in ((tb, fxt), (sb, fxs)):
                x = ref[k, rows(r, 8), :] + (0.5 * TIME_STEP) * west(keep[k])[:, BODY]
                ref[k, rows(r, 8), :] = jnp.where(kc > k, x, ZERO)
        return 0

    def out_copy(i, c):
        src = (ub, vb, tb, sb)[i]
        dst = (u_o, v_o, t_o, s_o)[i]
        at = pl.ds(pl.multiple_of(c * CH, CH), CH)
        frm = pl.ds(pl.multiple_of(c * CH + (8 if i else 0), 8), CH)
        return pltpu.make_async_copy(src.at[:, frm, :], dst.at[:, at, :], out_sem.at[i, c])

    def advect_chunk(c, _):
        lax.fori_loop(c * (CH // 8), (c + 1) * (CH // 8), advect, 0)
        for i in range(4):
            out_copy(i, c).start()
        return 0

    lax.fori_loop(0, NCH, advect_chunk, 0)

    def drain(c, _):
        for i in range(4):
            out_copy(i, c).wait()
        return 0

    lax.fori_loop(0, NCH, drain, 0)
    for c in planes:
        c.wait()


def vmem(*shape):
    return pltpu.VMEM(shape, F32)


def solution(mesh):
    any_spec = pl.BlockSpec(memory_space=pl.ANY)
    cube = jax.ShapeDtypeStruct((NL, NR, NC), F32)
    plane = jax.ShapeDtypeStruct((NR, NC), F32)

    tile, ghost, strip = vmem(NR, 128), vmem(ER, 128), vmem(NL, 8, NC)

    def arr(*shape):
        return jax.ShapeDtypeStruct(shape, F32)

    def local_step(vel_u, vel_v, temperature, salinity, sea_level, trans_u, trans_v, bathymetry, kmt_levels, tide_force):
        mid = pl.pallas_call(
            predict_kernel,
            name="predict",
            out_shape=(
                cube, cube, cube, cube, arr(9, ER, EC), arr(NR, 128), arr(NR, 128), arr(48, NC), arr(48, NC), arr(24, NC),
            ),
            in_specs=[any_spec] * 9,
            out_specs=(any_spec,) * 10,
            scratch_shapes=[
                *([vmem(NL, NR + 16, NC)] * 3), *([vmem(NL, NR, NC)] * 4),
                vmem(9, ER, EC), pltpu.VMEM((NR, NC), jnp.int32), vmem(NR, NC),
                *([tile] * 3), *([ghost] * 3), *([vmem(NL, NR + 16, 128)] * 3), vmem(NL, 8, EC), tile, vmem(NR + 16, 128),
                vmem(48, NC), vmem(72, NC), vmem(48, NC), vmem(72, NC),
                tile, vmem(48, NC), vmem(48, NC), tile, vmem(24, NC), vmem(NL, 8, EC), strip, strip,
                pltpu.SemaphoreType.DMA((4, NCH)), pltpu.SemaphoreType.DMA((5,)), pltpu.SemaphoreType.DMA((4, NCH)),
                pltpu.SemaphoreType.DMA((2,)), pltpu.SemaphoreType.DMA((25,)), pltpu.SemaphoreType.DMA((25,)),
            ],
            compiler_params=pltpu.CompilerParams(collective_id=0, has_side_effects=True, vmem_limit_bytes=63 * 2**20),
        )(vel_u, vel_v, temperature, salinity, sea_level, trans_u, trans_v, bathymetry, kmt_levels)
        return pl.pallas_call(
            finish_kernel,
            name="finish",
            out_shape=(plane, plane, plane, cube, cube, cube, cube),
            in_specs=[pl.BlockSpec(memory_space=pltpu.SMEM)] + [any_spec] * 10,
            out_specs=(any_spec,) * 7,
            scratch_shapes=[
                vmem(NL, NR, NC), vmem(NL, NR + 8, NC), vmem(NL, NR + 16, NC), vmem(NL, NR + 16, NC),
                vmem(9, ER, EC), vmem(2, ER, EC), vmem(2, ER, EC),
                vmem(NR, 128), vmem(NR, 128), vmem(48, NC), vmem(48, NC), vmem(24, NC), strip, strip,
                *([vmem(NL, 8, EC)] * 2), *([vmem(NL, NR, 128)] * 3),
                pltpu.SemaphoreType.DMA((4,)), pltpu.SemaphoreType.DMA((6,)), pltpu.SemaphoreType.DMA((4, NCH)),
                pltpu.SemaphoreType.DMA((3,)),
            ],
            compiler_params=pltpu.CompilerParams(vmem_limit_bytes=60 * 2**20),
        )(tide_force, *mid)

    spec_cube = P(None, "row", "col")
    spec_plane = P("row", "col")
    return jax.shard_map(
        local_step,
        mesh=mesh,
        in_specs=(spec_cube,) * 4 + (spec_plane,) * 5 + (P(None, None),),
        out_specs=(spec_plane,) * 3 + (spec_cube,) * 4,
        check_vma=False,
    )
```

time: 1210 us -> 81.4 us (0.07); the launches traced: 1190 us -> 81.2 us
  other arithmetic: 610 us -> 0 us
  starting transfers between devices: 259 us -> 0 us
  waiting for transfers between devices: 209 us -> 0 us
  local copies, waits for them, and re-layouts: 113 us -> 1.36 us
  Pallas kernels: 0 us -> 79.2 us
    dynamic_update_slice x160 -> x0, other arithmetic: 334 us -> none  [column_solve(): _, (gains, parts) = lax.scan(forward, start, (lower, diag, upper, source))]
    ppermute x135 -> x0, starting transfers between devices: 259 us -> none  [the longest x24 138 us: halo_swap(): from_south = lax.ppermute(wide[..., -1:, :], 'row', south_perm)]
    ppermute x135 -> x0, waiting for transfers between devices: 209 us -> none  [the longest x44 105 us: halo_swap(): from_east = lax.ppermute(field[..., :1], 'col', east_perm)]
    mul x34 -> x0, other arithmetic: 161 us -> none  [the longest x1 31.2 us: baroclinic_predict(): mask_u * (vel_um + TIME_STEP * tend_u)]
    pallas_call x0 -> x2, Pallas kernels: none -> 79.2 us  [the longest x1 49.5 us: local_step(): pl.pallas_call(predict_kernel, name='predict', out_shape=(cube, cube, cub...]
    another operation x13 -> x0, local copies, waits for them, and re-layouts: 39.5 us -> none
    concatenate x45 -> x0, other arithmetic: 36.6 us -> none  [the longest x3 31.9 us: column_solve(): lower = jnp.concatenate([edge, couple], axis=0)]
    slice x47 -> x0, local copies, waits for them, and re-layouts: 31.3 us -> none  [the longest x45 24 us: halo_swap(): from_west = lax.ppermute(field[..., -1:], 'col', west_perm)]
  transfers between devices with their start and end apart: 135 -> 0, of which waited for: 122 -> 0; matrix products, arithmetic and copies ran while one was open for 7% -> 0% of each run, Pallas kernels for 0% -> 0%
where the time goes in v1:
time: 81.4 us; the launch traced here: 81.2 us
  Pallas kernels  79.2 us (97%)
  local copies, waits for them, and re-layouts  1.36 us (2%)
    pallas_call x1, Pallas kernels, local_step(): pl.pallas_call(predict_kernel, name='predict', out_shape=(cube, cube, cub...  49.5 us
    pallas_call x1, Pallas kernels, local_step(): pl.pallas_call(finish_kernel, name='finish', out_shape=(plane, plane, pla...  29.7 us

profile of v1, /device:TPU:0, one launch (start us, length us, event | category | flops | bytes accessed | tf_op | source)
XLA Modules:
  0.0 81.2 jit_solution(4569476516416300811)
XLA Ops:
  0.6 1.4 %copy.17.tide = f32[20,2]{1,0:T(8,128)} copy(f32[20,2]{0,1:T(2,128)} %param.19) | data formatting | bytes 320 | tf_op args[9]
  2.0 49.5 %predict.1 = (f32[20,128,512]{2,1,0:T(8,128)}, f32[20,128,512]{2,1,0:T(8,128)}, f32[20,128,512]{2,1,0:T(8,128)}, f32[20,128,512]{2,1,0:T(8,128)}, f32[9,176,640]...) custom-call(f32[20,128,512]{2,1,0:T(8,128)} %u_h.1, ...), custom_call_target="tpu_custom_call" | custom-call | tf_op jit(solution)/shard_map/predict/pallas_call | solution.py:652
  51.5 29.7 %finish.1 = (f32[128,512]{1,0:T(8,128)}, f32[128,512]{1,0:T(8,128)}, f32[128,512]{1,0:T(8,128)}, f32[20,128,512]{2,1,0:T(8,128)}, f32[20,128,512]{2,1,0:T(8,128)...) custom-call(f32[20,2]{1,0:T(8,128)} %copy.17.tide, f32[20,128,512]{2,1,0:T(8,128)} %get-tuple-element.17.su_h, ...), custom_call_target="tpu_custom_call" | custom-call | tf_op jit(solution)/shard_map/finish/pallas_call | solution.py:671

commit v2 on v1

--- a/solution.py
+++ b/solution.py
@@ -18,8 +18,9 @@
 NR, NC = 128, 512
 HR = 24
 ER, EC = NR + 2 * HR, NC + 128
-NCH = 4
+NCH = 8
 CH = NR // NCH
+EARLY = NCH // 2
 DTB = TIME_STEP / NSUB
 F32 = jnp.float32
 ZERO = 0.0
@@ -28,6 +29,7 @@
 RIGHT = slice(NC - 128, NC)
 GHOST = slice(NC, EC)
 KMT, DZ, ETA, TU, TV, FX, FY, SV, SU = range(9)
+KU, KV, DU, DV = range(4)
 WIDE = 42
 MESH = pl.DeviceIdType.MESH
 
@@ -103,23 +105,18 @@
 
 
 def unpack_wide(tile, q):
-    lane = iota((8, 128), 1)
+    lane = iota(tile.shape, 1)
     moved = pltpu.roll(tile, 128 - WIDE * q, 1) if q else tile
     return jnp.where((lane < WIDE // 2) | (lane >= 128 - WIDE // 2), moved, ZERO)
 
 
 def solve(refs, masked, count, coef, gains, at):
-    low = gain = None
+    low = None
+    rest = 1.0
     parts = [None] * len(refs)
     for k in range(NL):
-        up = jnp.where(count > k + 1.0, coef, ZERO) if k < NL - 1 else None
-        if k == 0:
-            pivot = 1.0 + up
-        elif k < NL - 1:
-            pivot = (1.0 + up) + low * (1.0 - gain)
-        else:
-            pivot = 1.0 + low * (1.0 - gain)
-        inv = 1.0 / pivot
+        up = jnp.where(count > k + 1.0, coef, ZERO) if k < NL - 1 else ZERO
+        inv = 1.0 / (rest + up)
         for i, ref in enumerate(refs):
             src = ref[k, at, :]
             if not masked:
@@ -130,6 +127,7 @@
         if k < NL - 1:
             gain = up * inv
             gains[k] = gain
+            rest = 1.0 + gain * rest
         low = up
     for i, ref in enumerate(refs):
         ref[NL - 1, at, :] = parts[i]
@@ -143,7 +141,7 @@
 def predict_kernel(
     u_h, v_h, t_h, s_h, eta_h, tu_h, tv_h, dep_h, kmt_h,
     su_o, sv_o, tm_o, sm_o, ext_o, gts_o, gu_o, grts_o, grtn_o, grv_o,
-    ub, vb, pb, tb, sb, su, sv, ext, ktmp, htmp, pa, pb_, pc, ga, gb, gc, ug, vg, pg, dup, sp, gx, prn, prs, grs, grn, sts, trn, trs, sug, vrn, fp, gains, gains2,
+    ub, vb, pb, tb, sb, su, sv, ext, ktmp, htmp, pa, pb_, pc, ga, gb, gc, ug, vg, pg, dup, sp, gx, prn, prs, grs, grn, sts, trn, trs, sug, vrn, fp, fsp, csp, geo, tot, gains, gains2,
     load_sem, small_sem, out_sem, outs_sem, send_sem, recv_sem,
 ):
     col = lax.axis_index("col")
@@ -199,7 +197,7 @@
 
     for c in small:
         c.wait()
-    def stage(r, _):
+    for r in range(NR // 8):
         kf = ktmp[rows(r), :].astype(F32)
         dz = htmp[rows(r), :] / jnp.maximum(kf, 1.0)
         ext[KMT, rows(r, HR), BODY] = kf
@@ -207,9 +205,6 @@
         eta, tu, tv = (ext[f, rows(r, HR), BODY] for f in (ETA, TU, TV))
         pa[rows(r), :] = pack_wide((kf, dz, eta))
         pb_[rows(r), :] = pack_wide((tu, tv))
-        return 0
-
-    lax.fori_loop(0, NR // 8, stage, 0)
     pl.semaphore_wait(barrier, 5)
 
     def send_ext(lo, n, tile, ghost, base):
@@ -228,13 +223,8 @@
         for c in copies:
             c.wait()
 
-        def body(t, _):
-            g = ghost[rows(t), :]
-            for q, f in enumerate(fields):
-                ext[f, rows(t), GHOST] = unpack_wide(g, q)
-            return 0
-
-        lax.fori_loop(0, ER // 8, body, 0)
+        for q, f in enumerate(fields):
+            ext[f, :, GHOST] = unpack_wide(ghost[...], q)
 
     first = send_ext(KMT, 3, pa, ga, 0)
     later = send_ext(TU, 2, pb_, gb, 5)
@@ -243,11 +233,13 @@
         kc = ext[KMT, rows(r, HR), BODY]
         dz = ext[DZ, rows(r, HR), BODY]
         total = jnp.zeros((8, NC), F32)
+        scale = TIME_STEP * dz
         for k in range(NL):
-            dens = BETA_S * (sb[k, rows(r), :] - 1.0) - ALPHA_T * (tb[k, rows(r), :] - 1.0)
-            dens = jnp.where(kc > k, dens, ZERO)
-            total = total + dens
-            pb[k, rows(r, 8), :] = dz * (total - 0.5 * dens)
+            half = (0.5 * BETA_S) * (sb[k, rows(r), :] - 1.0) - (0.5 * ALPHA_T) * (tb[k, rows(r), :] - 1.0)
+            half = jnp.where(kc > k, half, ZERO)
+            middle = total + half
+            total = middle + half
+            pb[k, rows(r, 8), :] = scale * middle
         return 0
 
     def pressure_chunk(c, _):
@@ -257,6 +249,34 @@
         return 0
 
     lax.fori_loop(0, NCH, pressure_chunk, 0)
+
+    def out_copy(i, c):
+        src = (tb, sb, su, sv)[i]
+        dst = (tm_o, sm_o, su_o, sv_o)[i]
+        at = pl.ds(pl.multiple_of(c * CH, CH), CH)
+        return pltpu.make_async_copy(src.at[:, at, :], dst.at[:, at, :], out_sem.at[i, c])
+
+    def pack_ts(r):
+        tiles = []
+        for slot, ref in enumerate((tb, sb)):
+            for k in range(NL):
+                tiles.append((slot, k, ref[k, rows(r), LEFT], ref[k, rows(r), RIGHT]))
+        sts[rows(r), :] = pack(tiles)
+
+    def mix(r, _):
+        pack_ts(jnp.maximum(r - 1, 0))
+        kc = ext[KMT, rows(r, HR), BODY]
+        dz = ext[DZ, rows(r, HR), BODY]
+        solve((tb, sb), False, kc, (TIME_STEP * DIFF_KT) / (dz * dz), gains, rows(r))
+        return 0
+
+    def mix_chunk(c, _):
+        lax.fori_loop(c * (CH // 8), (c + 1) * (CH // 8), mix, 0)
+        out_copy(0, c).start()
+        out_copy(1, c).start()
+        return 0
+
+    lax.fori_loop(0, EARLY, mix_chunk, 0)
 
     receive_ext(first, ga, (KMT, DZ, ETA))
     has_south = (row > 0).astype(F32)
@@ -264,25 +284,32 @@
     ext[KMT, 0:HR, :] = ext[KMT, 0:HR, :] * has_south
     ext[KMT, HR + NR :, :] = ext[KMT, HR + NR :, :] * has_north
 
-    def count_u(r):
-        kc = ext[KMT, rows(r, HR), :]
-        return jnp.minimum(kc, east(kc))[:, BODY]
-
-    def count_v(r):
-        kc = ext[KMT, rows(r, HR), BODY]
-        return jnp.minimum(kc, north(kc, ext[KMT, rows(r, HR + 8), BODY]))
-
-    def mask_pack(r, _):
-        counts = (count_u(r), count_v(r))
+    for r in range(NR // 8):
+        at, above = rows(r, HR), rows(r, HR + 8)
+        kc, dz = ext[KMT, at, :], ext[DZ, at, :]
+        k_c, dz_c = kc[:, BODY], dz[:, BODY]
+        geo[KU, rows(r), :] = jnp.minimum(k_c, east(kc)[:, BODY])
+        geo[KV, rows(r), :] = jnp.minimum(k_c, north(k_c, ext[KMT, above, BODY]))
+        geo[DU, rows(r), :] = 0.5 * (dz_c + east(dz)[:, BODY])
+        geo[DV, rows(r), :] = 0.5 * (dz_c + north(dz_c, ext[DZ, above, BODY]))
+
+    def pack_uvp(r):
         tiles = []
         for slot, ref in enumerate((ub, vb, pb)):
             for k in range(NL):
-                x = ref[k, rows(r, 8), :]
-                if slot < 2:
-                    x = jnp.where(counts[slot] > k, x, ZERO)
-                    ref[k, rows(r, 8), :] = x
-                tiles.append((slot, k, x[:, LEFT], x[:, RIGHT]))
+                tiles.append((slot, k, ref[k, rows(r, 8), LEFT], ref[k, rows(r, 8), RIGHT]))
         sp[rows(r), :] = pack(tiles)
+
+    def mask_pack(r, _):
+        pack_uvp(jnp.maximum(r - 1, 0))
+        for slot, ref in enumerate((ub, vb)):
+            count = geo[slot, rows(r), :]
+            total = jnp.zeros((8, NC), F32)
+            for k in range(NL):
+                x = jnp.where(count > k, ref[k, rows(r, 8), :], ZERO)
+                ref[k, rows(r, 8), :] = x
+                total = total + x
+            tot[slot, rows(r), :] = total
         return 0
 
     def mask_chunk(c, _):
@@ -292,6 +319,7 @@
         return 0
 
     lax.fori_loop(0, NCH, mask_chunk, 0)
+    pack_uvp(NR // 8 - 1)
 
     def edge_row(dst, i, k, ref, at):
         dst[24 * i + k : 24 * i + k + 1, :] = ref[k, at : at + 1, :]
@@ -312,30 +340,8 @@
         send(sp.at[pl.ds(0, 8), :], gx.at[pl.ds(NR + 8, 8), :], 14, to_ds),
     ]
 
-    def out_copy(i, c):
-        src = (tb, sb, su, sv)[i]
-        dst = (tm_o, sm_o, su_o, sv_o)[i]
-        at = pl.ds(pl.multiple_of(c * CH, CH), CH)
-        return pltpu.make_async_copy(src.at[:, at, :], dst.at[:, at, :], out_sem.at[i, c])
-
-    def mix(r, _):
-        kc = ext[KMT, rows(r, HR), BODY]
-        dz = ext[DZ, rows(r, HR), BODY]
-        solve((tb, sb), False, kc, (TIME_STEP * DIFF_KT) / (dz * dz), gains, rows(r))
-        tiles = []
-        for slot, ref in enumerate((tb, sb)):
-            for k in range(NL):
-                tiles.append((slot, k, ref[k, rows(r), LEFT], ref[k, rows(r), RIGHT]))
-        sts[rows(r), :] = pack(tiles)
-        return 0
-
-    def mix_chunk(c, _):
-        lax.fori_loop(c * (CH // 8), (c + 1) * (CH // 8), mix, 0)
-        out_copy(0, c).start()
-        out_copy(1, c).start()
-        return 0
-
-    lax.fori_loop(0, NCH, mix_chunk, 0)
+    lax.fori_loop(EARLY, NCH, mix_chunk, 0)
+    pack_ts(NR // 8 - 1)
     for k in range(NL):
         for i, ref in enumerate((tb, sb)):
             edge_row(trs, i, k, ref, 0)
@@ -345,14 +351,16 @@
     for c in second:
         c.wait()
 
-    def spread(s, _):
-        g = gx[rows(s), :]
-        for k in range(NL):
-            for slot, ref in enumerate((ug, vg, pg)):
-                ref[k, rows(s), :] = unpack(g, slot, k)
-        return 0
-
-    lax.fori_loop(0, NR // 8 + 2, spread, 0)
+    def spread(i, _):
+        for j in range(3):
+            at = rows(3 * i + j)
+            g = gx[at, :]
+            for k in range(NL):
+                for slot, ref in enumerate((ug, vg, pg)):
+                    ref[k, at, :] = unpack(g, slot, k)
+        return 0
+
+    lax.fori_loop(0, (NR // 8 + 2) // 3, spread, 0)
     for k in range(NL):
         for i, ref in enumerate((ub, vb)):
             ghost_row(ref, k, 7, grs, i)
@@ -360,72 +368,67 @@
             ghost_row(ref, k, NR + 8, grn, i)
 
     def corner(r, k):
-        here, above = ub[k, rows(r, 8), :], ub[k, rows(r, 16), :]
-        g_here, g_above = ug[k, rows(r, 8), :], ug[k, rows(r, 16), :]
-        u_e = jnp.concatenate([here, g_here], 1)
-        un_e = jnp.concatenate([north(here, above), north(g_here, g_above)], 1)
-        v = vb[k, rows(r, 8), :]
-        v_e = jnp.concatenate([v, vg[k, rows(r, 8), :]], 1)
-        f_e = 0.25 * ((v_e + east(v_e)) * (u_e + un_e))
-        return u_e, v, f_e
-
-    for k in range(NL):
-        fp[k] = corner(-1, k)[2]
-
-    def tendency(r, _):
+        here, below = rows(r, 8), rows(r)
+        u_e = jnp.concatenate([ub[k, here, :], ug[k, here, :]], 1)
+        v = vb[k, here, :]
+        u_s = south(u_e, jnp.concatenate([ub[k, below, :], ug[k, below, :]], 1))
+        v_s = south(
+            jnp.concatenate([v, vg[k, here, :]], 1), jnp.concatenate([vb[k, below, :], vg[k, below, :]], 1)
+        )
+        f_s = (v_s + east(v_s)) * (u_s + u_e)
+        p = pb[k, here, :]
+        c = v + v_s[:, BODY]
+        c = c * c + p
+        return u_e, p, f_s, c
+
+    for k in range(NL):
+        fsp[k], csp[k] = corner(NR // 8, k)[2:]
+
+    def tendency(i, _):
+        r = NR // 8 - 1 - i
+        at = rows(r)
         for k in range(NL):
-            u_e, v, f_e = corner(r, k)
-            f = f_e[:, BODY]
-            f_s = south(f, fp[k, :, BODY])
-            fp[k] = f_e
-            p = pb[k, rows(r, 8), :]
-            p_e = east(jnp.concatenate([p, pg[k, rows(r, 8), :]], 1))[:, BODY]
-            p_n = north(p, pb[k, rows(r, 16), :])
-            du = 0.5 * (u_e + east(u_e))
-            du = du * du
-            dup[k] = du
-            hi = 0.5 * (v + north(v, vb[k, rows(r, 16), :]))
-            lo = 0.5 * (v + south(v, vb[k, rows(r), :]))
-            su[k, rows(r), :] = (f_s - f) + ((p - p_e) - du[:, BODY])
-            sv[k, rows(r), :] = (lo * lo - hi * hi) + ((p - p_n) - f)
-        k_u, k_v = count_u(r), count_v(r)
-        acc_u = acc_v = sum_u = sum_v = jnp.zeros((8, NC), F32)
+            u_e, p, f_s, c = corner(r, k)
+            f = north(f_s, fsp[k])
+            c_n = north(c, csp[k])
+            fsp[k], csp[k] = f_s, c
+            d = u_e + west(u_e)
+            d = d * d + jnp.concatenate([p, pg[k, rows(r, 8), :]], 1)
+            fp[k], dup[k] = f, d
+            su[k, at, :] = (f_s - f)[:, BODY] + d[:, BODY]
+            sv[k, at, :] = (c - c_n) - f[:, BODY]
+        k_u, k_v = geo[KU, at, :], geo[KV, at, :]
+        sum_u = sum_v = jnp.zeros((8, NC), F32)
         for k in range(NL):
-            u, v = ub[k, rows(r, 8), :], vb[k, rows(r, 8), :]
-            t_u = jnp.where(k_u > k, su[k, rows(r), :] + west(dup[k])[:, BODY], ZERO)
-            t_v = jnp.where(k_v > k, sv[k, rows(r), :] + west(fp[k])[:, BODY], ZERO)
-            su[k, rows(r), :] = u + TIME_STEP * t_u
-            sv[k, rows(r), :] = v + TIME_STEP * t_v
-            acc_u, acc_v = acc_u + t_u, acc_v + t_v
+            t_u = su[k, at, :] - east(dup[k])[:, BODY]
+            t_v = sv[k, at, :] + west(fp[k])[:, BODY]
+            u = jnp.where(k_u > k, ub[k, rows(r, 8), :] + t_u, ZERO)
+            v = jnp.where(k_v > k, vb[k, rows(r, 8), :] + t_v, ZERO)
+            su[k, at, :], sv[k, at, :] = u, v
             sum_u, sum_v = sum_u + u, sum_v + v
-        dz_u, dz_v = face_dz(r)
-        f_x, f_y = dz_u * acc_u, dz_v * acc_v
-        s_u = dz_u * (sum_u + TIME_STEP * acc_u)
-        ext[FX, rows(r, HR), BODY] = f_x
-        ext[FY, rows(r, HR), BODY] = f_y
-        ext[SU, rows(r, HR), BODY] = s_u
-        ext[SV, rows(r, HR), BODY] = dz_v * (sum_v + TIME_STEP * acc_v)
-        pc[rows(r), :] = pack_wide((f_x, f_y, s_u))
-        return 0
-
-    def face_dz(r):
-        dz_e = ext[DZ, rows(r, HR), :]
-        dz = dz_e[:, BODY]
-        dz_u = 0.5 * (dz + east(dz_e)[:, BODY])
-        dz_v = 0.5 * (dz + north(dz, ext[DZ, rows(r, HR + 8), BODY]))
-        return dz_u, dz_v
+        dz_u, dz_v = geo[DU, at, :], geo[DV, at, :]
+        ext[FX, rows(r, HR), BODY] = (dz_u / TIME_STEP) * (sum_u - tot[KU, at, :])
+        ext[FY, rows(r, HR), BODY] = (dz_v / TIME_STEP) * (sum_v - tot[KV, at, :])
+        ext[SU, rows(r, HR), BODY] = dz_u * sum_u
+        ext[SV, rows(r, HR), BODY] = dz_v * sum_v
+        return 0
 
     lax.fori_loop(0, NR // 8, tendency, 0)
+    for r in range(NR // 8):
+        pc[rows(r), :] = pack_wide([ext[f, rows(r, HR), BODY] for f in (FX, FY, SU)])
     fourth = send_ext(FX, 3, pc, gc, 18)
     receive_ext(later, gb, (TU, TV))
     out_ext0 = pltpu.make_async_copy(ext.at[pl.ds(0, 5)], ext_o.at[pl.ds(0, 5)], outs_sem.at[0])
     out_ext0.start()
 
+    def pack_su(r):
+        sug[rows(r), :] = pack([(0, k, su[k, rows(r), LEFT], su[k, rows(r), RIGHT]) for k in range(NL)])
+
     def momentum(r, _):
-        dz_u, dz_v = face_dz(r)
-        solve((su,), True, count_u(r), (TIME_STEP * VISC_KV) / (dz_u * dz_u), gains, rows(r))
-        solve((sv,), True, count_v(r), (TIME_STEP * VISC_KV) / (dz_v * dz_v), gains2, rows(r))
-        sug[rows(r), :] = pack([(0, k, su[k, rows(r), LEFT], su[k, rows(r), RIGHT]) for k in range(NL)])
+        pack_su(jnp.maximum(r - 1, 0))
+        for i, (ref, keep) in enumerate(((su, gains), (sv, gains2))):
+            dz = geo[DU + i, rows(r), :]
+            solve((ref,), True, geo[i, rows(r), :], (TIME_STEP * VISC_KV) / (dz * dz), keep, rows(r))
         return 0
 
     def momentum_chunk(c, _):
@@ -435,6 +438,7 @@
         return 0
 
     lax.fori_loop(0, NCH, momentum_chunk, 0)
+    pack_su(NR // 8 - 1)
     for k in range(NL):
         edge_row(vrn, 0, k, sv, NR - 1)
     fifth = [send(sug, gu_o, 23, to_x), send(vrn, grv_o, 24, to_n)]
@@ -459,7 +463,7 @@
 def finish_kernel(
     tide, su_h, sv_h, tm_h, sm_h, ext_h, gts_h, gu_h, grts_h, grtn_h, grv_h,
     eta_o, tu_o, tv_o, u_o, v_o, t_o, s_o,
-    ub, vb, tb, sb, ext, cof, avg, gts, gu, grts, grtn, grv, fpt, fps, fxt, fxs, ug, tg, sg,
+    ub, vb, tb, sb, ext, cof, cnt, avg, gts, gu, grts, grtn, grv, fpt, fps, fxt, fxs, ug, tg, sg,
     load_sem, small_sem, out_sem, outs_sem,
 ):
     early = pltpu.make_async_copy(ext_h, ext, small_sem.at[0])
@@ -487,25 +491,21 @@
         k_v = jnp.minimum(kc, north(kc, kn))
         return kc, k_u, k_v, k_u * (0.5 * (dz + east(dz))), k_v * (0.5 * (dz + north(dz, dn)))
 
-    def prepare(t, _):
+    for t in range(ER // 8):
         at = rows(t)
-        kc, k_u, k_v, h_u, h_v = faces(at, rows(jnp.minimum(t + 1, ER // 8 - 1)))
-        cof[0, at, :] = (DTB * DTB) * h_u
-        cof[1, at, :] = (DTB * DTB) * h_v
-        for f in (FX, FY):
-            ext[f, at, :] = (DTB * DTB) * ext[f, at, :]
+        kc, k_u, k_v, h_u, h_v = faces(at, rows(min(t + 1, ER // 8 - 1)))
+        for i, (count, h) in enumerate(((k_u, h_u), (k_v, h_v))):
+            cof[i, at, :] = (DTB * DTB) * h
+            cnt[i, at, :] = count
+            ext[FX + i, at, :] = (DTB * DTB) * ext[FX + i, at, :]
+            avg[i, at, :] = jnp.zeros((8, EC), F32)
         for f, count, scale in ((ETA, kc, 1.0), (TU, k_u, DTB), (TV, k_v, DTB)):
             ext[f, at, :] = jnp.where(count > ZERO, scale * ext[f, at, :], ZERO)
-        for i in range(2):
-            avg[i, at, :] = jnp.zeros((8, EC), F32)
-        return 0
-
-    lax.fori_loop(0, ER // 8, prepare, 0)
 
     norm = 6.0 / (NSUB * (NSUB + 1) * (NSUB + 2)) / DTB
 
     def subcycle(n, _, lo, hi):
-        tide_x, tide_y = tide[n, 0], tide[n, 1]
+        tide_x, tide_y = tide[0, n], tide[1, n]
         weight = norm * ((n + 1) * (NSUB - n)).astype(F32)
         v_prev = ext[TV, rows(max(lo - 1, 0)), :]
         eta_prev = None
@@ -535,13 +535,10 @@
     lax.fori_loop(4, 12, functools.partial(subcycle, lo=1, hi=tiles - 1), 0)
     lax.fori_loop(12, NSUB, functools.partial(subcycle, lo=2, hi=tiles - 2), 0)
 
-    def unscale(r, _):
+    for r in range(NR // 8):
         at = rows(r, HR)
         for f in (TU, TV):
             ext[f, at, :] = (1.0 / DTB) * ext[f, at, :]
-        return 0
-
-    lax.fori_loop(0, NR // 8, unscale, 0)
     planes = [
         pltpu.make_async_copy(ext.at[2 + i, pl.ds(HR, NR), pl.ds(0, NC)], o, outs_sem.at[i])
         for i, o in enumerate((eta_o, tu_o, tv_o))
@@ -558,12 +555,15 @@
             ref[k, 7:8, :] = grts[24 * i + k : 24 * i + k + 1, :]
             ref[k, NR + 8 : NR + 9, :] = grtn[24 * i + k : 24 * i + k + 1, :]
 
+    for r in range(-1, NR // 8):
+        at = rows(r, HR)
+        for i, f in enumerate((SU, SV)):
+            h = cof[i, at, :]
+            avg[i, at, :] = (DTB * DTB) * (avg[i, at, :] - ext[f, at, :]) / jnp.where(h > ZERO, h, 1.0)
+
     def strip(r):
-        at, above = rows(r, HR), rows(r, HR + 8)
-        kc, k_u, k_v, h_u, h_v = faces(at, above)
-        d_u = (avg[0, at, :] - ext[SU, at, :]) / jnp.where(h_u > ZERO, h_u, 1.0)
-        d_v = (avg[1, at, BODY] - ext[SV, at, BODY]) / jnp.where(h_v > ZERO, h_v, 1.0)[:, BODY]
-        return kc[:, BODY], k_u, k_v[:, BODY], d_u, d_v
+        at = rows(r, HR)
+        return ext[KMT, at, BODY], cnt[0, at, :], cnt[1, at, BODY], avg[0, at, :], avg[1, at, BODY]
 
     def flux_y(r, k, k_v, d_v):
         vc = jnp.where(k_v > k, vb[k, rows(r, 8), :] + d_v, ZERO)
@@ -580,15 +580,16 @@
         fpt[k] = a
         fps[k] = b
 
-    def spread(r, _):
-        g_u, g_ts = gu[rows(r), :], gts[rows(r), :]
-        for k in range(NL):
-            ug[k, rows(r), :] = unpack(g_u, 0, k)
-            tg[k, rows(r), :] = unpack(g_ts, 0, k)
-            sg[k, rows(r), :] = unpack(g_ts, 1, k)
-        return 0
-
-    lax.fori_loop(0, NR // 8, spread, 0)
+    def spread(i, _):
+        for j in range(4):
+            at = rows(4 * i + j)
+            g_u, g_ts = gu[at, :], gts[at, :]
+            for k in range(NL):
+                for ref, g, slot in ((ug, g_u, 0), (tg, g_ts, 0), (sg, g_ts, 1)):
+                    ref[k, at, :] = unpack(g, slot, k)
+        return 0
+
+    lax.fori_loop(0, NR // 8 // 4, spread, 0)
 
     def advect(r, _):
         kc, k_u, k_v, d_u, d_v = strip(r)
@@ -662,7 +663,7 @@
                 vmem(9, ER, EC), pltpu.VMEM((NR, NC), jnp.int32), vmem(NR, NC),
                 *([tile] * 3), *([ghost] * 3), *([vmem(NL, NR + 16, 128)] * 3), vmem(NL, 8, EC), tile, vmem(NR + 16, 128),
                 vmem(48, NC), vmem(72, NC), vmem(48, NC), vmem(72, NC),
-                tile, vmem(48, NC), vmem(48, NC), tile, vmem(24, NC), vmem(NL, 8, EC), strip, strip,
+                tile, vmem(48, NC), vmem(48, NC), tile, vmem(24, NC), *([vmem(NL, 8, EC)] * 2), strip, vmem(4, NR, NC), vmem(2, NR, NC), strip, strip,
                 pltpu.SemaphoreType.DMA((4, NCH)), pltpu.SemaphoreType.DMA((5,)), pltpu.SemaphoreType.DMA((4, NCH)),
                 pltpu.SemaphoreType.DMA((2,)), pltpu.SemaphoreType.DMA((25,)), pltpu.SemaphoreType.DMA((25,)),
             ],
@@ -676,14 +677,14 @@
             out_specs=(any_spec,) * 7,
             scratch_shapes=[
                 vmem(NL, NR, NC), vmem(NL, NR + 8, NC), vmem(NL, NR + 16, NC), vmem(NL, NR + 16, NC),
-                vmem(9, ER, EC), vmem(2, ER, EC), vmem(2, ER, EC),
+                vmem(9, ER, EC), *([vmem(2, ER, EC)] * 3),
                 vmem(NR, 128), vmem(NR, 128), vmem(48, NC), vmem(48, NC), vmem(24, NC), strip, strip,
                 *([vmem(NL, 8, EC)] * 2), *([vmem(NL, NR, 128)] * 3),
                 pltpu.SemaphoreType.DMA((4,)), pltpu.SemaphoreType.DMA((6,)), pltpu.SemaphoreType.DMA((4, NCH)),
                 pltpu.SemaphoreType.DMA((3,)),
             ],
             compiler_params=pltpu.CompilerParams(vmem_limit_bytes=60 * 2**20),
-        )(tide_force, *mid)
+        )(tide_force.T, *mid)
 
     spec_cube = P(None, "row", "col")
     spec_plane = P("row", "col")

time: 81.4 us -> 68.6 us (0.84)
  Pallas kernels: 79.2 us -> 67.8 us
  local copies, waits for them, and re-layouts: 1.36 us -> 0 us
    pallas_call x1, Pallas kernels: 49.5 us -> 41.4 us  [local_step(): pl.pallas_call(predict_kernel, name='predict', out_shape=(cube, cube, cub...]
    pallas_call x1, Pallas kernels: 29.7 us -> 26.4 us  [local_step(): pl.pallas_call(finish_kernel, name='finish', out_shape=(plane, plane, pla...]
    unnamed x1 -> x0, local copies, waits for them, and re-layouts: 1.36 us -> none
where the time goes in v2:
time: 68.6 us; the launch traced here: 68.4 us
  Pallas kernels  67.8 us (99%)
    pallas_call x1, Pallas kernels, local_step(): pl.pallas_call(predict_kernel, name='predict', out_shape=(cube, cube, cub...  41.4 us
    pallas_call x1, Pallas kernels, local_step(): pl.pallas_call(finish_kernel, name='finish', out_shape=(plane, plane, pla...  26.4 us

profile of v2, /device:TPU:0, one launch (start us, length us, event | category | flops | bytes accessed | tf_op | source)
XLA Modules:
  0.0 68.4 jit_solution(4088725341385374754)
XLA Ops:
  0.6 41.4 %predict.1 = (f32[20,128,512]{2,1,0:T(8,128)}, f32[20,128,512]{2,1,0:T(8,128)}, f32[20,128,512]{2,1,0:T(8,128)}, f32[20,128,512]{2,1,0:T(8,128)}, f32[9,176,640]...) custom-call(f32[20,128,512]{2,1,0:T(8,128)} %u_h.1, ...), custom_call_target="tpu_custom_call" | custom-call | tf_op jit(solution)/shard_map/predict/pallas_call | solution.py:653
  42.1 26.4 %finish.1 = (f32[128,512]{1,0:T(8,128)}, f32[128,512]{1,0:T(8,128)}, f32[128,512]{1,0:T(8,128)}, f32[20,128,512]{2,1,0:T(8,128)}, f32[20,128,512]{2,1,0:T(8,128)...) custom-call(f32[2,20]{1,0:T(2,128)} %bitcast.1, f32[20,128,512]{2,1,0:T(8,128)} %get-tuple-element.17.su_h, ...), custom_call_target="tpu_custom_call" | custom-call | tf_op jit(solution)/shard_map/finish/pallas_call | solution.py:672

commit v3 on v2

--- a/solution.py
+++ b/solution.py
@@ -20,6 +20,7 @@
 ER, EC = NR + 2 * HR, NC + 128
 NCH = 8
 CH = NR // NCH
+STRIPS, PER, TILES = (n // 8 for n in (NR, CH, ER))
 EARLY = NCH // 2
 DTB = TIME_STEP / NSUB
 F32 = jnp.float32
@@ -34,6 +35,14 @@
 MESH = pl.DeviceIdType.MESH
 
 
+def loop(lo, hi, body):
+    def step(i, carry):
+        body(i)
+        return carry
+
+    lax.fori_loop(lo, hi, step, 0)
+
+
 def rows(r, off=0):
     start = 8 * r + off
     if isinstance(start, int):
@@ -59,6 +68,30 @@
 
 def south(here, below):
     return pltpu.roll(jnp.where(iota(here.shape, 0) == 7, below, here), 1, 0)
+
+
+def lane_tiles(x):
+    return [x[:, 128 * c : 128 * (c + 1)] for c in range(NC // 128)]
+
+
+def east_of(x, ghost):
+    moved = [pltpu.roll(t, 127, 1) for t in lane_tiles(x)] + [ghost]
+    last = iota((8, 128), 1) == 127
+    return jnp.concatenate([jnp.where(last, b, a) for a, b in zip(moved, moved[1:])], 1)
+
+
+def west_of(x, ghost):
+    moved = [ghost] + [pltpu.roll(t, 1, 1) for t in lane_tiles(x)]
+    first = iota((8, 128), 1) == 0
+    return jnp.concatenate([jnp.where(first, a, b) for a, b in zip(moved, moved[1:])], 1)
+
+
+def turn(x, by):
+    return pltpu.roll(x, by % 128, 1)
+
+
+def even_odd(a, b):
+    return jnp.where(iota((8, 128), 1) % 2 == 0, a, b)
 
 
 def lane_of(slot, k):
@@ -140,8 +173,8 @@
 
 def predict_kernel(
     u_h, v_h, t_h, s_h, eta_h, tu_h, tv_h, dep_h, kmt_h,
-    su_o, sv_o, tm_o, sm_o, ext_o, gts_o, gu_o, grts_o, grtn_o, grv_o,
-    ub, vb, pb, tb, sb, su, sv, ext, ktmp, htmp, pa, pb_, pc, ga, gb, gc, ug, vg, pg, dup, sp, gx, prn, prs, grs, grn, sts, trn, trs, sug, vrn, fp, fsp, csp, geo, tot, gains, gains2,
+    su_o, sv_o, tm_o, sm_o, ext_o, gts_o, gu_o, grts_o, grtn_o, grv_o, sts_o,
+    ub, vb, pb, tb, sb, su, sv, ext, ktmp, htmp, pa, pb_, pc, ga, gb, gc, pka, pkb, ga2, gb2, dup, sp, gx, prn, prs, grs, grn, sts, trn, trs, sug, vrn, fp, fsp, csp, geo, tot, gains, gains2,
     load_sem, small_sem, out_sem, outs_sem, send_sem, recv_sem,
 ):
     col = lax.axis_index("col")
@@ -178,12 +211,11 @@
         return pltpu.make_async_copy(src.at[:, at, :], dst.at[:, to, :], load_sem.at[i, c])
 
     def start_loads(pair):
-        def body(c, _):
+        def body(c):
             for i in pair:
                 load(i, c).start()
-            return 0
-
-        lax.fori_loop(0, NCH, body, 0)
+
+        loop(0, NCH, body)
 
     start_loads((0, 1))
     start_loads((2, 3))
@@ -197,7 +229,7 @@
 
     for c in small:
         c.wait()
-    for r in range(NR // 8):
+    for r in range(STRIPS):
         kf = ktmp[rows(r), :].astype(F32)
         dz = htmp[rows(r), :] / jnp.maximum(kf, 1.0)
         ext[KMT, rows(r, HR), BODY] = kf
@@ -229,7 +261,7 @@
     first = send_ext(KMT, 3, pa, ga, 0)
     later = send_ext(TU, 2, pb_, gb, 5)
 
-    def pressure(r, _):
+    def pressure(r):
         kc = ext[KMT, rows(r, HR), BODY]
         dz = ext[DZ, rows(r, HR), BODY]
         total = jnp.zeros((8, NC), F32)
@@ -240,15 +272,13 @@
             middle = total + half
             total = middle + half
             pb[k, rows(r, 8), :] = scale * middle
-        return 0
-
-    def pressure_chunk(c, _):
+
+    def pressure_chunk(c):
         load(0, c).wait()
         load(1, c).wait()
-        lax.fori_loop(c * (CH // 8), (c + 1) * (CH // 8), pressure, 0)
-        return 0
-
-    lax.fori_loop(0, NCH, pressure_chunk, 0)
+        loop(c * (PER), (c + 1) * (PER), pressure)
+
+    loop(0, NCH, pressure_chunk)
 
     def out_copy(i, c):
         src = (tb, sb, su, sv)[i]
@@ -263,20 +293,18 @@
                 tiles.append((slot, k, ref[k, rows(r), LEFT], ref[k, rows(r), RIGHT]))
         sts[rows(r), :] = pack(tiles)
 
-    def mix(r, _):
+    def mix(r):
         pack_ts(jnp.maximum(r - 1, 0))
         kc = ext[KMT, rows(r, HR), BODY]
         dz = ext[DZ, rows(r, HR), BODY]
         solve((tb, sb), False, kc, (TIME_STEP * DIFF_KT) / (dz * dz), gains, rows(r))
-        return 0
-
-    def mix_chunk(c, _):
-        lax.fori_loop(c * (CH // 8), (c + 1) * (CH // 8), mix, 0)
+
+    def mix_chunk(c):
+        loop(c * (PER), (c + 1) * (PER), mix)
         out_copy(0, c).start()
         out_copy(1, c).start()
-        return 0
-
-    lax.fori_loop(0, EARLY, mix_chunk, 0)
+
+    loop(0, EARLY, mix_chunk)
 
     receive_ext(first, ga, (KMT, DZ, ETA))
     has_south = (row > 0).astype(F32)
@@ -284,7 +312,7 @@
     ext[KMT, 0:HR, :] = ext[KMT, 0:HR, :] * has_south
     ext[KMT, HR + NR :, :] = ext[KMT, HR + NR :, :] * has_north
 
-    for r in range(NR // 8):
+    for r in range(STRIPS):
         at, above = rows(r, HR), rows(r, HR + 8)
         kc, dz = ext[KMT, at, :], ext[DZ, at, :]
         k_c, dz_c = kc[:, BODY], dz[:, BODY]
@@ -297,11 +325,44 @@
         tiles = []
         for slot, ref in enumerate((ub, vb, pb)):
             for k in range(NL):
-                tiles.append((slot, k, ref[k, rows(r, 8), LEFT], ref[k, rows(r, 8), RIGHT]))
-        sp[rows(r), :] = pack(tiles)
-
-    def mask_pack(r, _):
-        pack_uvp(jnp.maximum(r - 1, 0))
+                x = [ref[k, rows(r, 8), LEFT], ref[k, rows(r, 8), RIGHT]]
+                if slot < 2:
+                    x = [jnp.where(geo[slot, rows(r), at] > k, t, ZERO) for t, at in zip(x, (LEFT, RIGHT))]
+                tiles.append((slot, k, *x))
+        sp[rows(r, 8), :] = pack(tiles)
+
+    def pack_chunk(c):
+        load(2, c).wait()
+        load(3, c).wait()
+        loop(c * (PER), (c + 1) * (PER), pack_uvp)
+
+    loop(0, NCH, pack_chunk)
+
+    def edge_row(dst, i, k, ref, at):
+        dst[24 * i + k : 24 * i + k + 1, :] = ref[k, at : at + 1, :]
+
+    def ghost_row(ref, k, at, src, i):
+        ref[k, at : at + 1, :] = src[24 * i + k : 24 * i + k + 1, :]
+
+    def masked_row(dst, i, k, ref, r):
+        dst[24 * i + k : 24 * i + k + 1, :] = jnp.where(geo[i, r : r + 1, :] > k, ref[k, r + 8 : r + 9, :], ZERO)
+
+    for k in range(NL):
+        for i, ref in enumerate((ub, vb)):
+            masked_row(prs, i, k, ref, 0)
+            masked_row(prn, i, k, ref, NR - 1)
+        edge_row(prs, 2, k, pb, 8)
+    low, high = pl.ds(8, 8), pl.ds(NR, 8)
+    second = [
+        send(sp.at[pl.ds(8, NR), :], gx.at[pl.ds(8, NR), :], 10, to_x),
+        send(prn, grs, 11, to_n),
+        send(prs, grn, 12, to_s),
+        send(sp.at[high, :], gx.at[pl.ds(0, 8), :], 13, to_dn),
+        send(sp.at[low, :], gx.at[pl.ds(NR + 8, 8), :], 14, to_ds),
+        send(sp.at[high, :], sp.at[pl.ds(0, 8), :], 25, to_n),
+    ]
+
+    def mask(r):
         for slot, ref in enumerate((ub, vb)):
             count = geo[slot, rows(r), :]
             total = jnp.zeros((8, NC), F32)
@@ -310,38 +371,10 @@
                 ref[k, rows(r, 8), :] = x
                 total = total + x
             tot[slot, rows(r), :] = total
-        return 0
-
-    def mask_chunk(c, _):
-        load(2, c).wait()
-        load(3, c).wait()
-        lax.fori_loop(c * (CH // 8), (c + 1) * (CH // 8), mask_pack, 0)
-        return 0
-
-    lax.fori_loop(0, NCH, mask_chunk, 0)
-    pack_uvp(NR // 8 - 1)
-
-    def edge_row(dst, i, k, ref, at):
-        dst[24 * i + k : 24 * i + k + 1, :] = ref[k, at : at + 1, :]
-
-    def ghost_row(ref, k, at, src, i):
-        ref[k, at : at + 1, :] = src[24 * i + k : 24 * i + k + 1, :]
-
-    for k in range(NL):
-        for i, ref in enumerate((ub, vb, pb)):
-            edge_row(prs, i, k, ref, 8)
-        for i, ref in enumerate((ub, vb)):
-            edge_row(prn, i, k, ref, NR + 7)
-    second = [
-        send(sp, gx.at[pl.ds(8, NR), :], 10, to_x),
-        send(prn, grs, 11, to_n),
-        send(prs, grn, 12, to_s),
-        send(sp.at[pl.ds(NR - 8, 8), :], gx.at[pl.ds(0, 8), :], 13, to_dn),
-        send(sp.at[pl.ds(0, 8), :], gx.at[pl.ds(NR + 8, 8), :], 14, to_ds),
-    ]
-
-    lax.fori_loop(EARLY, NCH, mix_chunk, 0)
-    pack_ts(NR // 8 - 1)
+
+    loop(0, STRIPS, mask)
+    loop(EARLY, NCH, mix_chunk)
+    pack_ts(STRIPS - 1)
     for k in range(NL):
         for i, ref in enumerate((tb, sb)):
             edge_row(trs, i, k, ref, 0)
@@ -351,57 +384,63 @@
     for c in second:
         c.wait()
 
-    def spread(i, _):
-        for j in range(3):
-            at = rows(3 * i + j)
-            g = gx[at, :]
+    corner_w = None
+    for t in range(STRIPS + 1, 0, -1):
+        g, own = gx[rows(t), :], sp[rows(t), :]
+        g_s, own_s = south(g, gx[rows(t - 1), :]), south(own, sp[rows(t - 1), :])
+        pka[rows(t - 1), :] = even_odd(turn(g, 1), turn(g_s, -41))
+        flux = (turn(g_s, -39) + turn(own_s, -40)) * turn(g_s + g, 1)
+        if corner_w is not None:
+            d = own + turn(g, -1)
+            pkb[rows(t - 1), :] = even_odd(north(flux, corner_w), d * d + turn(g, -81))
+        corner_w = flux
+
+    def spread(i):
+        for j in range(4):
+            at = rows(4 * i + j)
+            a, b = pka[at, :], pkb[at, :]
             for k in range(NL):
-                for slot, ref in enumerate((ug, vg, pg)):
-                    ref[k, at, :] = unpack(g, slot, k)
-        return 0
-
-    lax.fori_loop(0, (NR // 8 + 2) // 3, spread, 0)
+                ga2[k, at, :] = unpack(a, 0, k)
+                gb2[k, at, :] = unpack(b, 0, k)
+
+    loop(0, STRIPS // 4, spread)
     for k in range(NL):
         for i, ref in enumerate((ub, vb)):
             ghost_row(ref, k, 7, grs, i)
         for i, ref in enumerate((ub, vb, pb)):
             ghost_row(ref, k, NR + 8, grn, i)
 
-    def corner(r, k):
-        here, below = rows(r, 8), rows(r)
-        u_e = jnp.concatenate([ub[k, here, :], ug[k, here, :]], 1)
-        v = vb[k, here, :]
-        u_s = south(u_e, jnp.concatenate([ub[k, below, :], ug[k, below, :]], 1))
-        v_s = south(
-            jnp.concatenate([v, vg[k, here, :]], 1), jnp.concatenate([vb[k, below, :], vg[k, below, :]], 1)
-        )
-        f_s = (v_s + east(v_s)) * (u_s + u_e)
-        p = pb[k, here, :]
-        c = v + v_s[:, BODY]
-        c = c * c + p
-        return u_e, p, f_s, c
+    def corner(r, k, ghost):
+        u, v, p = (ref[k, rows(r, 8), :] for ref in (ub, vb, pb))
+        u_s = south(u, ub[k, rows(r), :])
+        v_s = south(v, vb[k, rows(r), :])
+        f_s = (v_s + east_of(v_s, ghost)) * (u_s + u)
+        c = v + v_s
+        return u, p, f_s, c * c + p
 
     for k in range(NL):
-        fsp[k], csp[k] = corner(NR // 8, k)[2:]
-
-    def tendency(i, _):
-        r = NR // 8 - 1 - i
+        fsp[k], csp[k] = corner(STRIPS, k, unpack(pka[NR : NR + 8, :], 0, k))[2:]
+
+    def tendency(i):
+        r = STRIPS - 1 - i
         at = rows(r)
         for k in range(NL):
-            u_e, p, f_s, c = corner(r, k)
+            ghost = ga2[k, at, :]
+            u, p, f_s, c = corner(r, k, ghost)
             f = north(f_s, fsp[k])
             c_n = north(c, csp[k])
             fsp[k], csp[k] = f_s, c
-            d = u_e + west(u_e)
-            d = d * d + jnp.concatenate([p, pg[k, rows(r, 8), :]], 1)
+            d = u + west_of(u, ghost)
+            d = d * d + p
             fp[k], dup[k] = f, d
-            su[k, at, :] = (f_s - f)[:, BODY] + d[:, BODY]
-            sv[k, at, :] = (c - c_n) - f[:, BODY]
+            su[k, at, :] = (f_s - f) + d
+            sv[k, at, :] = (c - c_n) - f
         k_u, k_v = geo[KU, at, :], geo[KV, at, :]
         sum_u = sum_v = jnp.zeros((8, NC), F32)
         for k in range(NL):
-            t_u = su[k, at, :] - east(dup[k])[:, BODY]
-            t_v = sv[k, at, :] + west(fp[k])[:, BODY]
+            ghost = gb2[k, at, :]
+            t_u = su[k, at, :] - east_of(dup[k], ghost)
+            t_v = sv[k, at, :] + west_of(fp[k], ghost)
             u = jnp.where(k_u > k, ub[k, rows(r, 8), :] + t_u, ZERO)
             v = jnp.where(k_v > k, vb[k, rows(r, 8), :] + t_v, ZERO)
             su[k, at, :], sv[k, at, :] = u, v
@@ -411,66 +450,75 @@
         ext[FY, rows(r, HR), BODY] = (dz_v / TIME_STEP) * (sum_v - tot[KV, at, :])
         ext[SU, rows(r, HR), BODY] = dz_u * sum_u
         ext[SV, rows(r, HR), BODY] = dz_v * sum_v
-        return 0
-
-    lax.fori_loop(0, NR // 8, tendency, 0)
-    for r in range(NR // 8):
+
+    loop(0, STRIPS, tendency)
+    for r in range(STRIPS):
         pc[rows(r), :] = pack_wide([ext[f, rows(r, HR), BODY] for f in (FX, FY, SU)])
     fourth = send_ext(FX, 3, pc, gc, 18)
     receive_ext(later, gb, (TU, TV))
     out_ext0 = pltpu.make_async_copy(ext.at[pl.ds(0, 5)], ext_o.at[pl.ds(0, 5)], outs_sem.at[0])
     out_ext0.start()
 
+    def implicit(i, ref, keep, r):
+        dz = geo[DU + i, rows(r), :]
+        solve((ref,), True, geo[i, rows(r), :], (TIME_STEP * VISC_KV) / (dz * dz), keep, rows(r))
+
     def pack_su(r):
         sug[rows(r), :] = pack([(0, k, su[k, rows(r), LEFT], su[k, rows(r), RIGHT]) for k in range(NL)])
 
-    def momentum(r, _):
+    def solve_u(r):
         pack_su(jnp.maximum(r - 1, 0))
-        for i, (ref, keep) in enumerate(((su, gains), (sv, gains2))):
-            dz = geo[DU + i, rows(r), :]
-            solve((ref,), True, geo[i, rows(r), :], (TIME_STEP * VISC_KV) / (dz * dz), keep, rows(r))
-        return 0
-
-    def momentum_chunk(c, _):
-        lax.fori_loop(c * (CH // 8), (c + 1) * (CH // 8), momentum, 0)
+        implicit(0, su, gains, r)
+
+    def solve_v(r):
+        implicit(1, sv, gains2, r)
+
+    def u_chunk(c):
+        loop(c * (PER), (c + 1) * (PER), solve_u)
         out_copy(2, c).start()
+
+    def v_chunk(c):
+        loop(c * (PER), jnp.minimum((c + 1) * (PER), STRIPS - 1), solve_v)
         out_copy(3, c).start()
-        return 0
-
-    lax.fori_loop(0, NCH, momentum_chunk, 0)
-    pack_su(NR // 8 - 1)
+
+    solve_v(STRIPS - 1)
+    loop(0, NCH, u_chunk)
+    pack_su(STRIPS - 1)
     for k in range(NL):
         edge_row(vrn, 0, k, sv, NR - 1)
     fifth = [send(sug, gu_o, 23, to_x), send(vrn, grv_o, 24, to_n)]
+    loop(0, NCH, v_chunk)
     receive_ext(fourth, gc, (FX, FY, SU))
     out_ext1 = pltpu.make_async_copy(ext.at[pl.ds(5, 4)], ext_o.at[pl.ds(5, 4)], outs_sem.at[1])
     out_ext1.start()
-
-    def drain(c, _):
+    out_sts = pltpu.make_async_copy(sts, sts_o, outs_sem.at[2])
+    out_sts.start()
+
+    def drain(c):
         for i in range(4):
             out_copy(i, c).wait()
-        return 0
-
-    lax.fori_loop(0, NCH, drain, 0)
+
+    loop(0, NCH, drain)
     for c in third:
         c.wait()
     for c in fifth:
         c.wait()
     out_ext0.wait()
     out_ext1.wait()
+    out_sts.wait()
 
 
 def finish_kernel(
-    tide, su_h, sv_h, tm_h, sm_h, ext_h, gts_h, gu_h, grts_h, grtn_h, grv_h,
+    tide, su_h, sv_h, tm_h, sm_h, ext_h, gts_h, gu_h, grts_h, grtn_h, grv_h, sts_h,
     eta_o, tu_o, tv_o, u_o, v_o, t_o, s_o,
-    ub, vb, tb, sb, ext, cof, cnt, avg, gts, gu, grts, grtn, grv, fpt, fps, fxt, fxs, ug, tg, sg,
+    ub, vb, tb, sb, ext, cof, cnt, avg, gts, gu, grts, grtn, grv, sts, fpt, fps, fxt, fxs, pkt, tg, sg,
     load_sem, small_sem, out_sem, outs_sem,
 ):
     early = pltpu.make_async_copy(ext_h, ext, small_sem.at[0])
     early.start()
     small = [
         pltpu.make_async_copy(a, b, small_sem.at[i + 1])
-        for i, (a, b) in enumerate(((gts_h, gts), (gu_h, gu), (grts_h, grts), (grtn_h, grtn), (grv_h, grv)))
+        for i, (a, b) in enumerate(((gts_h, gts), (gu_h, gu), (grts_h, grts), (grtn_h, grtn), (grv_h, grv), (sts_h, sts)))
     ]
     for c in small:
         c.start()
@@ -491,9 +539,9 @@
         k_v = jnp.minimum(kc, north(kc, kn))
         return kc, k_u, k_v, k_u * (0.5 * (dz + east(dz))), k_v * (0.5 * (dz + north(dz, dn)))
 
-    for t in range(ER // 8):
+    for t in range(TILES):
         at = rows(t)
-        kc, k_u, k_v, h_u, h_v = faces(at, rows(min(t + 1, ER // 8 - 1)))
+        kc, k_u, k_v, h_u, h_v = faces(at, rows(min(t + 1, TILES - 1)))
         for i, (count, h) in enumerate(((k_u, h_u), (k_v, h_v))):
             cof[i, at, :] = (DTB * DTB) * h
             cnt[i, at, :] = count
@@ -504,7 +552,7 @@
 
     norm = 6.0 / (NSUB * (NSUB + 1) * (NSUB + 2)) / DTB
 
-    def subcycle(n, _, lo, hi):
+    def subcycle(n, lo, hi):
         tide_x, tide_y = tide[0, n], tide[1, n]
         weight = norm * ((n + 1) * (NSUB - n)).astype(F32)
         v_prev = ext[TV, rows(max(lo - 1, 0)), :]
@@ -528,14 +576,13 @@
                     avg[0, b, :] = avg[0, b, :] + weight * u_new
                     avg[1, b, :] = avg[1, b, :] + weight * v_new
             eta_prev, u_keep, v_keep, v_prev = eta, u, v, v
-        return 0
-
-    tiles = ER // 8
-    lax.fori_loop(0, 4, functools.partial(subcycle, lo=0, hi=tiles), 0)
-    lax.fori_loop(4, 12, functools.partial(subcycle, lo=1, hi=tiles - 1), 0)
-    lax.fori_loop(12, NSUB, functools.partial(subcycle, lo=2, hi=tiles - 2), 0)
-
-    for r in range(NR // 8):
+
+    tiles = TILES
+    loop(0, 4, functools.partial(subcycle, lo=0, hi=tiles))
+    loop(4, 12, functools.partial(subcycle, lo=1, hi=tiles - 1))
+    loop(12, NSUB, functools.partial(subcycle, lo=2, hi=tiles - 2))
+
+    for r in range(STRIPS):
         at = rows(r, HR)
         for f in (TU, TV):
             ext[f, at, :] = (1.0 / DTB) * ext[f, at, :]
@@ -555,7 +602,7 @@
             ref[k, 7:8, :] = grts[24 * i + k : 24 * i + k + 1, :]
             ref[k, NR + 8 : NR + 9, :] = grtn[24 * i + k : 24 * i + k + 1, :]
 
-    for r in range(-1, NR // 8):
+    for r in range(-1, STRIPS):
         at = rows(r, HR)
         for i, f in enumerate((SU, SV)):
             h = cof[i, at, :]
@@ -563,7 +610,7 @@
 
     def strip(r):
         at = rows(r, HR)
-        return ext[KMT, at, BODY], cnt[0, at, :], cnt[1, at, BODY], avg[0, at, :], avg[1, at, BODY]
+        return [x[at, BODY] for x in (ext.at[KMT], cnt.at[0], cnt.at[1], avg.at[0], avg.at[1])]
 
     def flux_y(r, k, k_v, d_v):
         vc = jnp.where(k_v > k, vb[k, rows(r, 8), :] + d_v, ZERO)
@@ -580,35 +627,42 @@
         fpt[k] = a
         fps[k] = b
 
-    def spread(i, _):
+    lane = iota((8, 128), 1)
+    level = (((lane + 1) % 128) // 2).astype(F32)
+    for r in range(STRIPS):
+        at = rows(r, HR)
+        count, add = (jnp.broadcast_to(x[0, at, EC - 1 : EC], (8, 128)) for x in (cnt, avg))
+        uc = jnp.where(count > level, gu[rows(r), :] + add, ZERO)
+        uc = jnp.where((lane < 39) | (lane == 127), uc, turn(uc, 40))
+        g = gts[rows(r), :]
+        pkt[rows(r), :] = even_odd(turn(uc * (g + turn(sts[rows(r), :], -1)), 1), turn(g, -1))
+
+    def spread(i):
         for j in range(4):
             at = rows(4 * i + j)
-            g_u, g_ts = gu[at, :], gts[at, :]
+            g = pkt[at, :]
             for k in range(NL):
-                for ref, g, slot in ((ug, g_u, 0), (tg, g_ts, 0), (sg, g_ts, 1)):
-                    ref[k, at, :] = unpack(g, slot, k)
-        return 0
-
-    lax.fori_loop(0, NR // 8 // 4, spread, 0)
-
-    def advect(r, _):
+                tg[k, at, :] = unpack(g, 0, k)
+                sg[k, at, :] = unpack(g, 1, k)
+
+    loop(0, STRIPS // 4, spread)
+
+    def advect(r):
         kc, k_u, k_v, d_u, d_v = strip(r)
         for k in range(NL):
             vc, t, y_t, s, y_s = flux_y(r, k, k_v, d_v)
             vb[k, rows(r, 8), :] = vc
-            uc = jnp.where(k_u > k, jnp.concatenate([ub[k, rows(r), :], ug[k, rows(r), :]], 1) + d_u, ZERO)
-            ub[k, rows(r), :] = uc[:, BODY]
+            uc = jnp.where(k_u > k, ub[k, rows(r), :] + d_u, ZERO)
+            ub[k, rows(r), :] = uc
             for ref, ghost, prev, keep, x, y in ((tb, tg, fpt, fxt, t, y_t), (sb, sg, fps, fxs, s, y_s)):
-                x_e = jnp.concatenate([x, ghost[k, rows(r), :]], 1)
-                fx = uc * (x_e + east(x_e))
+                fx = uc * (x + east_of(x, ghost[k, rows(r), :]))
                 keep[k] = fx
-                ref[k, rows(r, 8), :] = x - (0.5 * TIME_STEP) * (fx[:, BODY] + (y - south(y, prev[k])))
+                ref[k, rows(r, 8), :] = x - (0.5 * TIME_STEP) * (fx + (y - south(y, prev[k])))
                 prev[k] = y
         for k in range(NL):
-            for ref, keep in ((tb, fxt), (sb, fxs)):
-                x = ref[k, rows(r, 8), :] + (0.5 * TIME_STEP) * west(keep[k])[:, BODY]
+            for ref, ghost, keep in ((tb, tg, fxt), (sb, sg, fxs)):
+                x = ref[k, rows(r, 8), :] + (0.5 * TIME_STEP) * west_of(keep[k], ghost[k, rows(r), :])
                 ref[k, rows(r, 8), :] = jnp.where(kc > k, x, ZERO)
-        return 0
 
     def out_copy(i, c):
         src = (ub, vb, tb, sb)[i]
@@ -617,20 +671,18 @@
         frm = pl.ds(pl.multiple_of(c * CH + (8 if i else 0), 8), CH)
         return pltpu.make_async_copy(src.at[:, frm, :], dst.at[:, at, :], out_sem.at[i, c])
 
-    def advect_chunk(c, _):
-        lax.fori_loop(c * (CH // 8), (c + 1) * (CH // 8), advect, 0)
+    def advect_chunk(c):
+        loop(c * (PER), (c + 1) * (PER), advect)
         for i in range(4):
             out_copy(i, c).start()
-        return 0
-
-    lax.fori_loop(0, NCH, advect_chunk, 0)
-
-    def drain(c, _):
+
+    loop(0, NCH, advect_chunk)
+
+    def drain(c):
         for i in range(4):
             out_copy(i, c).wait()
-        return 0
-
-    lax.fori_loop(0, NCH, drain, 0)
+
+    loop(0, NCH, drain)
     for c in planes:
         c.wait()
 
@@ -655,17 +707,18 @@
             name="predict",
             out_shape=(
                 cube, cube, cube, cube, arr(9, ER, EC), arr(NR, 128), arr(NR, 128), arr(48, NC), arr(48, NC), arr(24, NC),
+                arr(NR, 128),
             ),
             in_specs=[any_spec] * 9,
-            out_specs=(any_spec,) * 10,
+            out_specs=(any_spec,) * 11,
             scratch_shapes=[
                 *([vmem(NL, NR + 16, NC)] * 3), *([vmem(NL, NR, NC)] * 4),
                 vmem(9, ER, EC), pltpu.VMEM((NR, NC), jnp.int32), vmem(NR, NC),
-                *([tile] * 3), *([ghost] * 3), *([vmem(NL, NR + 16, 128)] * 3), vmem(NL, 8, EC), tile, vmem(NR + 16, 128),
+                *([tile] * 3), *([ghost] * 3), vmem(NR + 8, 128), tile, *([vmem(NL, NR, 128)] * 2), strip, *([vmem(NR + 16, 128)] * 2),
                 vmem(48, NC), vmem(72, NC), vmem(48, NC), vmem(72, NC),
-                tile, vmem(48, NC), vmem(48, NC), tile, vmem(24, NC), *([vmem(NL, 8, EC)] * 2), strip, vmem(4, NR, NC), vmem(2, NR, NC), strip, strip,
+                tile, vmem(48, NC), vmem(48, NC), tile, vmem(24, NC), *([strip] * 3), vmem(4, NR, NC), vmem(2, NR, NC), strip, strip,
                 pltpu.SemaphoreType.DMA((4, NCH)), pltpu.SemaphoreType.DMA((5,)), pltpu.SemaphoreType.DMA((4, NCH)),
-                pltpu.SemaphoreType.DMA((2,)), pltpu.SemaphoreType.DMA((25,)), pltpu.SemaphoreType.DMA((25,)),
+                pltpu.SemaphoreType.DMA((3,)), pltpu.SemaphoreType.DMA((26,)), pltpu.SemaphoreType.DMA((26,)),
             ],
             compiler_params=pltpu.CompilerParams(collective_id=0, has_side_effects=True, vmem_limit_bytes=63 * 2**20),
         )(vel_u, vel_v, temperature, salinity, sea_level, trans_u, trans_v, bathymetry, kmt_levels)
@@ -673,14 +726,13 @@
             finish_kernel,
             name="finish",
             out_shape=(plane, plane, plane, cube, cube, cube, cube),
-            in_specs=[pl.BlockSpec(memory_space=pltpu.SMEM)] + [any_spec] * 10,
+            in_specs=[pl.BlockSpec(memory_space=pltpu.SMEM)] + [any_spec] * 11,
             out_specs=(any_spec,) * 7,
             scratch_shapes=[
                 vmem(NL, NR, NC), vmem(NL, NR + 8, NC), vmem(NL, NR + 16, NC), vmem(NL, NR + 16, NC),
                 vmem(9, ER, EC), *([vmem(2, ER, EC)] * 3),
-                vmem(NR, 128), vmem(NR, 128), vmem(48, NC), vmem(48, NC), vmem(24, NC), strip, strip,
-                *([vmem(NL, 8, EC)] * 2), *([vmem(NL, NR, 128)] * 3),
-                pltpu.SemaphoreType.DMA((4,)), pltpu.SemaphoreType.DMA((6,)), pltpu.SemaphoreType.DMA((4, NCH)),
+                vmem(NR, 128), vmem(NR, 128), vmem(48, NC), vmem(48, NC), vmem(24, NC), tile, *([strip] * 4), tile, *([vmem(NL, NR, 128)] * 2),
+                pltpu.SemaphoreType.DMA((4,)), pltpu.SemaphoreType.DMA((7,)), pltpu.SemaphoreType.DMA((4, NCH)),
                 pltpu.SemaphoreType.DMA((3,)),
             ],
             compiler_params=pltpu.CompilerParams(vmem_limit_bytes=60 * 2**20),

time: 68.6 us -> 65.1 us (0.949)
  Pallas kernels: 67.8 us -> 64.4 us
    pallas_call x1, Pallas kernels: 41.4 us -> 39.3 us  [local_step(): pl.pallas_call(predict_kernel, name='predict', out_shape=(cube, cube, cub...]
    pallas_call x1, Pallas kernels: 26.4 us -> 25 us  [local_step(): pl.pallas_call(finish_kernel, name='finish', out_shape=(plane, plane, pla...]
where the time goes in v3:
time: 65.1 us; the launch traced here: 65 us
  Pallas kernels  64.4 us (99%)
    pallas_call x1, Pallas kernels, local_step(): pl.pallas_call(predict_kernel, name='predict', out_shape=(cube, cube, cub...  39.3 us
    pallas_call x1, Pallas kernels, local_step(): pl.pallas_call(finish_kernel, name='finish', out_shape=(plane, plane, pla...  25 us

profile of v3, /device:TPU:0, one launch (start us, length us, event | category | flops | bytes accessed | tf_op | source)
XLA Modules:
  0.0 65.0 jit_solution(6051450650051357670)
XLA Ops:
  0.6 39.3 %predict.1 = (f32[20,128,512]{2,1,0:T(8,128)}, f32[20,128,512]{2,1,0:T(8,128)}, f32[20,128,512]{2,1,0:T(8,128)}, f32[20,128,512]{2,1,0:T(8,128)}, f32[9,176,640]...) custom-call(f32[20,128,512]{2,1,0:T(8,128)} %u_h.1, ...), custom_call_target="tpu_custom_call" | custom-call | tf_op jit(solution)/shard_map/predict/pallas_call | solution.py:705
  40.0 25.0 %finish.1 = (f32[128,512]{1,0:T(8,128)}, f32[128,512]{1,0:T(8,128)}, f32[128,512]{1,0:T(8,128)}, f32[20,128,512]{2,1,0:T(8,128)}, f32[20,128,512]{2,1,0:T(8,128)...) custom-call(f32[2,20]{1,0:T(2,128)} %bitcast.1, f32[20,128,512]{2,1,0:T(8,128)} %get-tuple-element.18.su_h, ...), custom_call_target="tpu_custom_call" | custom-call | tf_op jit(solution)/shard_map/finish/pallas_call | solution.py:725

commit v4 on v3

--- a/solution.py
+++ b/solution.py
@@ -18,11 +18,14 @@
 NR, NC = 128, 512
 HR = 24
 ER, EC = NR + 2 * HR, NC + 128
-NCH = 8
+NCH = 16
 CH = NR // NCH
-STRIPS, PER, TILES = (n // 8 for n in (NR, CH, ER))
-EARLY = NCH // 2
+STRIPS, TILES = NR // 8, ER // 8
+PAIR, TRIPLE = 2, 3
+NORTH = 2 * PAIR
+EARLY = 4
 DTB = TIME_STEP / NSUB
+HALF_DT = 0.5 * TIME_STEP
 F32 = jnp.float32
 ZERO = 0.0
 BODY = slice(0, NC)
@@ -35,12 +38,13 @@
 MESH = pl.DeviceIdType.MESH
 
 
-def loop(lo, hi, body):
+def loop(lo, hi, body, per=1):
     def step(i, carry):
-        body(i)
+        for j in range(per):
+            body(lo + per * i + j)
         return carry
 
-    lax.fori_loop(lo, hi, step, 0)
+    lax.fori_loop(0, (hi - lo) // per, step, 0)
 
 
 def rows(r, off=0):
@@ -141,6 +145,12 @@
     lane = iota(tile.shape, 1)
     moved = pltpu.roll(tile, 128 - WIDE * q, 1) if q else tile
     return jnp.where((lane < WIDE // 2) | (lane >= 128 - WIDE // 2), moved, ZERO)
+
+
+def packed_lanes():
+    lane = iota((8, 128), 1)
+    in_first = (lane < 39) | (lane == 127)
+    return lane, in_first, jnp.where(lane == 127, ZERO, (((lane + 1) % 40) // 2).astype(F32))
 
 
 def solve(refs, masked, count, coef, gains, at):
@@ -174,7 +184,7 @@
 def predict_kernel(
     u_h, v_h, t_h, s_h, eta_h, tu_h, tv_h, dep_h, kmt_h,
     su_o, sv_o, tm_o, sm_o, ext_o, gts_o, gu_o, grts_o, grtn_o, grv_o, sts_o,
-    ub, vb, pb, tb, sb, su, sv, ext, ktmp, htmp, pa, pb_, pc, ga, gb, gc, pka, pkb, ga2, gb2, dup, sp, gx, prn, prs, grs, grn, sts, trn, trs, sug, vrn, fp, fsp, csp, geo, tot, gains, gains2,
+    ub, vb, pb, tb, sb, su, sv, ext, ktmp, htmp, pa, pb_, pc, ga, gb, gc, pka, pkb, ga2, gb2, dup, sp, gx, prn, prs, grs, grn, sts, trn, trs, sug, vrn, fp, fsp, csp, geo, wet_g, wet_o, tot, gains, gains2,
     load_sem, small_sem, out_sem, outs_sem, send_sem, recv_sem,
 ):
     col = lax.axis_index("col")
@@ -221,12 +231,16 @@
     start_loads((2, 3))
 
     def send(src, dst, idx, dev):
-        c = pltpu.make_async_remote_copy(
+        c = remote(src, dst, idx, dev)
+        c.start()
+        return c
+
+    def remote(src, dst, idx, dev):
+        return pltpu.make_async_remote_copy(
             src_ref=src, dst_ref=dst, send_sem=send_sem.at[idx], recv_sem=recv_sem.at[idx], device_id=dev, device_id_type=MESH
         )
-        c.start()
-        return c
-
+
+    lane, in_first, level = packed_lanes()
     for c in small:
         c.wait()
     for r in range(STRIPS):
@@ -239,17 +253,22 @@
         pb_[rows(r), :] = pack_wide((tu, tv))
     pl.semaphore_wait(barrier, 5)
 
+    def start(copies):
+        for c in copies:
+            c.start()
+
     def send_ext(lo, n, tile, ghost, base):
         at = pl.ds(lo, n)
         low, high, mid = pl.ds(0, HR), pl.ds(HR + NR, HR), pl.ds(HR, NR)
         body = pl.ds(0, NC)
-        return [
-            send(tile, ghost.at[mid, :], base, to_x),
-            send(ext.at[at, pl.ds(NR, HR), body], ext.at[at, low, body], base + 1, to_n),
-            send(ext.at[at, pl.ds(HR, HR), body], ext.at[at, high, body], base + 2, to_s),
-            send(tile.at[pl.ds(NR - HR, HR), :], ghost.at[low, :], base + 3, to_dn),
-            send(tile.at[low, :], ghost.at[high, :], base + 4, to_ds),
-        ]
+        parts = (
+            (ext.at[at, pl.ds(NR, HR), body], ext.at[at, low, body], to_n),
+            (tile.at[pl.ds(NR - HR, HR), :], ghost.at[low, :], to_dn),
+            (tile, ghost.at[mid, :], to_x),
+            (ext.at[at, pl.ds(HR, HR), body], ext.at[at, high, body], to_s),
+            (tile.at[low, :], ghost.at[high, :], to_ds),
+        )
+        return [remote(a, b, base + i, dev) for i, (a, b, dev) in enumerate(parts)]
 
     def receive_ext(copies, ghost, fields):
         for c in copies:
@@ -259,7 +278,7 @@
             ext[f, :, GHOST] = unpack_wide(ghost[...], q)
 
     first = send_ext(KMT, 3, pa, ga, 0)
-    later = send_ext(TU, 2, pb_, gb, 5)
+    start(first)
 
     def pressure(r):
         kc = ext[KMT, rows(r, HR), BODY]
@@ -276,9 +295,8 @@
     def pressure_chunk(c):
         load(0, c).wait()
         load(1, c).wait()
-        loop(c * (PER), (c + 1) * (PER), pressure)
-
-    loop(0, NCH, pressure_chunk)
+        pressure(c)
+
 
     def out_copy(i, c):
         src = (tb, sb, su, sv)[i]
@@ -300,58 +318,44 @@
         solve((tb, sb), False, kc, (TIME_STEP * DIFF_KT) / (dz * dz), gains, rows(r))
 
     def mix_chunk(c):
-        loop(c * (PER), (c + 1) * (PER), mix)
+        mix(c)
         out_copy(0, c).start()
         out_copy(1, c).start()
 
-    loop(0, EARLY, mix_chunk)
-
-    receive_ext(first, ga, (KMT, DZ, ETA))
-    has_south = (row > 0).astype(F32)
-    has_north = (row < n_row - 1).astype(F32)
-    ext[KMT, 0:HR, :] = ext[KMT, 0:HR, :] * has_south
-    ext[KMT, HR + NR :, :] = ext[KMT, HR + NR :, :] * has_north
-
-    for r in range(STRIPS):
-        at, above = rows(r, HR), rows(r, HR + 8)
-        kc, dz = ext[KMT, at, :], ext[DZ, at, :]
-        k_c, dz_c = kc[:, BODY], dz[:, BODY]
-        geo[KU, rows(r), :] = jnp.minimum(k_c, east(kc)[:, BODY])
-        geo[KV, rows(r), :] = jnp.minimum(k_c, north(k_c, ext[KMT, above, BODY]))
-        geo[DU, rows(r), :] = 0.5 * (dz_c + east(dz)[:, BODY])
-        geo[DV, rows(r), :] = 0.5 * (dz_c + north(dz_c, ext[DZ, above, BODY]))
+    def both_chunk(c):
+        pressure_chunk(c)
+        mix_chunk(c)
+
+    loop(0, EARLY, both_chunk, PAIR)
+    loop(EARLY, NCH, pressure_chunk, PAIR)
 
     def pack_uvp(r):
         tiles = []
         for slot, ref in enumerate((ub, vb, pb)):
             for k in range(NL):
                 x = [ref[k, rows(r, 8), LEFT], ref[k, rows(r, 8), RIGHT]]
-                if slot < 2:
-                    x = [jnp.where(geo[slot, rows(r), at] > k, t, ZERO) for t, at in zip(x, (LEFT, RIGHT))]
                 tiles.append((slot, k, *x))
         sp[rows(r, 8), :] = pack(tiles)
 
     def pack_chunk(c):
         load(2, c).wait()
         load(3, c).wait()
-        loop(c * (PER), (c + 1) * (PER), pack_uvp)
-
-    loop(0, NCH, pack_chunk)
+        pack_uvp(c)
+
+    loop(0, NCH, pack_chunk, PAIR)
 
     def edge_row(dst, i, k, ref, at):
         dst[24 * i + k : 24 * i + k + 1, :] = ref[k, at : at + 1, :]
 
     def ghost_row(ref, k, at, src, i):
-        ref[k, at : at + 1, :] = src[24 * i + k : 24 * i + k + 1, :]
-
-    def masked_row(dst, i, k, ref, r):
-        dst[24 * i + k : 24 * i + k + 1, :] = jnp.where(geo[i, r : r + 1, :] > k, ref[k, r + 8 : r + 9, :], ZERO)
+        x = src[24 * i + k : 24 * i + k + 1, :]
+        ref[k, at : at + 1, :] = jnp.where(geo[i, at : at + 1, :] > k, x, ZERO) if i < 2 else x
 
     for k in range(NL):
-        for i, ref in enumerate((ub, vb)):
-            masked_row(prs, i, k, ref, 0)
-            masked_row(prn, i, k, ref, NR - 1)
-        edge_row(prs, 2, k, pb, 8)
+        for i, ref in enumerate((ub, vb, pb)):
+            edge_row(prs, i, k, ref, 8)
+            if i < 2:
+                edge_row(prn, i, k, ref, NR + 7)
     low, high = pl.ds(8, 8), pl.ds(NR, 8)
     second = [
         send(sp.at[pl.ds(8, NR), :], gx.at[pl.ds(8, NR), :], 10, to_x),
@@ -362,9 +366,43 @@
         send(sp.at[high, :], sp.at[pl.ds(0, 8), :], 25, to_n),
     ]
 
+    later = send_ext(TU, 2, pb_, gb, 5)
+    start(later)
+
+    loop(EARLY, NCH, mix_chunk, PAIR)
+    pack_ts(STRIPS - 1)
+    for k in range(NL):
+        for i, ref in enumerate((tb, sb)):
+            edge_row(trs, i, k, ref, 0)
+            edge_row(trn, i, k, ref, NR - 1)
+    third = [send(sts, gts_o, 15, to_x), send(trn, grts_o, 16, to_n), send(trs, grtn_o, 17, to_s)]
+
+    receive_ext(first, ga, (KMT, DZ, ETA))
+    has_south = (row > 0).astype(F32)
+    has_north = (row < n_row - 1).astype(F32)
+    ext[KMT, 0:HR, :] = ext[KMT, 0:HR, :] * has_south
+    ext[KMT, HR + NR :, :] = ext[KMT, HR + NR :, :] * has_north
+
+    for r in range(-1, STRIPS + 1):
+        at, above = rows(r, HR), rows(r, HR + 8)
+        kc, dz = ext[KMT, at, :], ext[DZ, at, :]
+        k_u = jnp.minimum(kc, east(kc))
+        k_v = jnp.minimum(kc, north(kc, ext[KMT, above, :]))
+        geo[KU, rows(r, 8), :] = k_u[:, BODY]
+        geo[KV, rows(r, 8), :] = k_v[:, BODY]
+        geo[DU, rows(r, 8), :] = 0.5 * (dz + east(dz))[:, BODY]
+        geo[DV, rows(r, 8), :] = 0.5 * (dz + north(dz, ext[DZ, above, :]))[:, BODY]
+        (u_w, u_e, u_l), (v_w, v_e, v_f) = (
+            [jnp.broadcast_to(x[:, i : i + 1], (8, 128)) for i in at]
+            for x, at in ((k_u, (EC - 1, NC, NC - 1)), (k_v, (EC - 1, NC, 0)))
+        )
+        top = jnp.where(lane < 2 * 40 - 1, even_odd(v_e, v_w), 1.0 * NL)
+        wet_g[rows(r, 8), :] = jnp.where(in_first, even_odd(u_e, u_w), top)
+        wet_o[rows(r, 8), :] = jnp.where(in_first, u_l, v_f)
+
     def mask(r):
         for slot, ref in enumerate((ub, vb)):
-            count = geo[slot, rows(r), :]
+            count = geo[slot, rows(r, 8), :]
             total = jnp.zeros((8, NC), F32)
             for k in range(NL):
                 x = jnp.where(count > k, ref[k, rows(r, 8), :], ZERO)
@@ -372,22 +410,17 @@
                 total = total + x
             tot[slot, rows(r), :] = total
 
-    loop(0, STRIPS, mask)
-    loop(EARLY, NCH, mix_chunk)
-    pack_ts(STRIPS - 1)
-    for k in range(NL):
-        for i, ref in enumerate((tb, sb)):
-            edge_row(trs, i, k, ref, 0)
-            edge_row(trn, i, k, ref, NR - 1)
-    third = [send(sts, gts_o, 15, to_x), send(trn, grts_o, 16, to_n), send(trs, grtn_o, 17, to_s)]
-
+    loop(0, STRIPS, mask, PAIR)
     for c in second:
         c.wait()
 
+    def wet(x, count, t):
+        return jnp.where(count[rows(t), :] > level, x[rows(t), :], ZERO)
+
     corner_w = None
     for t in range(STRIPS + 1, 0, -1):
-        g, own = gx[rows(t), :], sp[rows(t), :]
-        g_s, own_s = south(g, gx[rows(t - 1), :]), south(own, sp[rows(t - 1), :])
+        g, own, below = wet(gx, wet_g, t), wet(sp, wet_o, t), t - 1
+        g_s, own_s = south(g, wet(gx, wet_g, below)), south(own, wet(sp, wet_o, below))
         pka[rows(t - 1), :] = even_odd(turn(g, 1), turn(g_s, -41))
         flux = (turn(g_s, -39) + turn(own_s, -40)) * turn(g_s + g, 1)
         if corner_w is not None:
@@ -435,7 +468,7 @@
             fp[k], dup[k] = f, d
             su[k, at, :] = (f_s - f) + d
             sv[k, at, :] = (c - c_n) - f
-        k_u, k_v = geo[KU, at, :], geo[KV, at, :]
+        k_u, k_v, dz_u, dz_v = (geo[i, rows(r, 8), :] for i in (KU, KV, DU, DV))
         sum_u = sum_v = jnp.zeros((8, NC), F32)
         for k in range(NL):
             ghost = gb2[k, at, :]
@@ -445,23 +478,36 @@
             v = jnp.where(k_v > k, vb[k, rows(r, 8), :] + t_v, ZERO)
             su[k, at, :], sv[k, at, :] = u, v
             sum_u, sum_v = sum_u + u, sum_v + v
-        dz_u, dz_v = geo[DU, at, :], geo[DV, at, :]
         ext[FX, rows(r, HR), BODY] = (dz_u / TIME_STEP) * (sum_u - tot[KU, at, :])
         ext[FY, rows(r, HR), BODY] = (dz_v / TIME_STEP) * (sum_v - tot[KV, at, :])
         ext[SU, rows(r, HR), BODY] = dz_u * sum_u
         ext[SV, rows(r, HR), BODY] = dz_v * sum_v
 
-    loop(0, STRIPS, tendency)
-    for r in range(STRIPS):
-        pc[rows(r), :] = pack_wide([ext[f, rows(r, HR), BODY] for f in (FX, FY, SU)])
+    def pack_forcing(lo, hi):
+        for r in range(lo, hi):
+            pc[rows(r), :] = pack_wide([ext[f, rows(r, HR), BODY] for f in (FX, FY, SU)])
+
     fourth = send_ext(FX, 3, pc, gc, 18)
+
+    def leave_north():
+        pack_forcing(STRIPS - NORTH, STRIPS)
+        start(fourth[:2])
+
+    def tendency_pair(i):
+        for j in range(PAIR):
+            tendency(PAIR * i + j)
+        pl.when(i == NORTH // PAIR - 1)(leave_north)
+
+    loop(0, STRIPS // PAIR, tendency_pair)
+    pack_forcing(0, STRIPS - NORTH)
+    start(fourth[2:])
     receive_ext(later, gb, (TU, TV))
     out_ext0 = pltpu.make_async_copy(ext.at[pl.ds(0, 5)], ext_o.at[pl.ds(0, 5)], outs_sem.at[0])
     out_ext0.start()
 
     def implicit(i, ref, keep, r):
-        dz = geo[DU + i, rows(r), :]
-        solve((ref,), True, geo[i, rows(r), :], (TIME_STEP * VISC_KV) / (dz * dz), keep, rows(r))
+        dz = geo[DU + i, rows(r, 8), :]
+        solve((ref,), True, geo[i, rows(r, 8), :], (TIME_STEP * VISC_KV) / (dz * dz), keep, rows(r))
 
     def pack_su(r):
         sug[rows(r), :] = pack([(0, k, su[k, rows(r), LEFT], su[k, rows(r), RIGHT]) for k in range(NL)])
@@ -474,23 +520,31 @@
         implicit(1, sv, gains2, r)
 
     def u_chunk(c):
-        loop(c * (PER), (c + 1) * (PER), solve_u)
+        solve_u(c)
         out_copy(2, c).start()
 
     def v_chunk(c):
-        loop(c * (PER), jnp.minimum((c + 1) * (PER), STRIPS - 1), solve_v)
+        solve_v(c)
         out_copy(3, c).start()
 
-    solve_v(STRIPS - 1)
-    loop(0, NCH, u_chunk)
+    v_chunk(NCH - 1)
+    loop(0, NCH, u_chunk, PAIR)
     pack_su(STRIPS - 1)
     for k in range(NL):
         edge_row(vrn, 0, k, sv, NR - 1)
     fifth = [send(sug, gu_o, 23, to_x), send(vrn, grv_o, 24, to_n)]
-    loop(0, NCH, v_chunk)
-    receive_ext(fourth, gc, (FX, FY, SU))
     out_ext1 = pltpu.make_async_copy(ext.at[pl.ds(5, 4)], ext_o.at[pl.ds(5, 4)], outs_sem.at[1])
-    out_ext1.start()
+
+    def take_forcing():
+        receive_ext(fourth, gc, (FX, FY, SU))
+        out_ext1.start()
+
+    def v_triple(i):
+        for j in range(TRIPLE):
+            v_chunk(TRIPLE * i + j)
+        pl.when(i == TRIPLE - 1)(take_forcing)
+
+    loop(0, STRIPS // TRIPLE, v_triple)
     out_sts = pltpu.make_async_copy(sts, sts_o, outs_sem.at[2])
     out_sts.start()
 
@@ -514,12 +568,16 @@
     ub, vb, tb, sb, ext, cof, cnt, avg, gts, gu, grts, grtn, grv, sts, fpt, fps, fxt, fxs, pkt, tg, sg,
     load_sem, small_sem, out_sem, outs_sem,
 ):
-    early = pltpu.make_async_copy(ext_h, ext, small_sem.at[0])
+    early, late = (
+        pltpu.make_async_copy(ext_h.at[at], ext.at[at], small_sem.at[i])
+        for i, at in enumerate((pl.ds(KMT, SV), pl.ds(SV, 2)))
+    )
     early.start()
     small = [
-        pltpu.make_async_copy(a, b, small_sem.at[i + 1])
+        pltpu.make_async_copy(a, b, small_sem.at[i + 2])
         for i, (a, b) in enumerate(((gts_h, gts), (gu_h, gu), (grts_h, grts), (grtn_h, grtn), (grv_h, grv), (sts_h, sts)))
     ]
+    late.start()
     for c in small:
         c.start()
     big = [
@@ -592,6 +650,7 @@
     ]
     for c in planes:
         c.start()
+    late.wait()
     for c in small:
         c.wait()
     for c in big:
@@ -627,13 +686,12 @@
         fpt[k] = a
         fps[k] = b
 
-    lane = iota((8, 128), 1)
-    level = (((lane + 1) % 128) // 2).astype(F32)
+    _, in_first, level = packed_lanes()
     for r in range(STRIPS):
         at = rows(r, HR)
         count, add = (jnp.broadcast_to(x[0, at, EC - 1 : EC], (8, 128)) for x in (cnt, avg))
         uc = jnp.where(count > level, gu[rows(r), :] + add, ZERO)
-        uc = jnp.where((lane < 39) | (lane == 127), uc, turn(uc, 40))
+        uc = jnp.where(in_first, uc, turn(uc, 40))
         g = gts[rows(r), :]
         pkt[rows(r), :] = even_odd(turn(uc * (g + turn(sts[rows(r), :], -1)), 1), turn(g, -1))
 
@@ -657,11 +715,11 @@
             for ref, ghost, prev, keep, x, y in ((tb, tg, fpt, fxt, t, y_t), (sb, sg, fps, fxs, s, y_s)):
                 fx = uc * (x + east_of(x, ghost[k, rows(r), :]))
                 keep[k] = fx
-                ref[k, rows(r, 8), :] = x - (0.5 * TIME_STEP) * (fx + (y - south(y, prev[k])))
+                ref[k, rows(r, 8), :] = x - HALF_DT * (fx + (y - south(y, prev[k])))
                 prev[k] = y
         for k in range(NL):
             for ref, ghost, keep in ((tb, tg, fxt), (sb, sg, fxs)):
-                x = ref[k, rows(r, 8), :] + (0.5 * TIME_STEP) * west_of(keep[k], ghost[k, rows(r), :])
+                x = ref[k, rows(r, 8), :] + HALF_DT * west_of(keep[k], ghost[k, rows(r), :])
                 ref[k, rows(r, 8), :] = jnp.where(kc > k, x, ZERO)
 
     def out_copy(i, c):
@@ -672,11 +730,11 @@
         return pltpu.make_async_copy(src.at[:, frm, :], dst.at[:, at, :], out_sem.at[i, c])
 
     def advect_chunk(c):
-        loop(c * (PER), (c + 1) * (PER), advect)
+        advect(c)
         for i in range(4):
             out_copy(i, c).start()
 
-    loop(0, NCH, advect_chunk)
+    loop(0, NCH, advect_chunk, PAIR)
 
     def drain(c):
         for i in range(4):
@@ -716,7 +774,7 @@
                 vmem(9, ER, EC), pltpu.VMEM((NR, NC), jnp.int32), vmem(NR, NC),
                 *([tile] * 3), *([ghost] * 3), vmem(NR + 8, 128), tile, *([vmem(NL, NR, 128)] * 2), strip, *([vmem(NR + 16, 128)] * 2),
                 vmem(48, NC), vmem(72, NC), vmem(48, NC), vmem(72, NC),
-                tile, vmem(48, NC), vmem(48, NC), tile, vmem(24, NC), *([strip] * 3), vmem(4, NR, NC), vmem(2, NR, NC), strip, strip,
+                tile, vmem(48, NC), vmem(48, NC), tile, vmem(24, NC), *([strip] * 3), vmem(4, NR + 16, NC), *([vmem(NR + 16, 128)] * 2), vmem(2, NR, NC), strip, strip,
                 pltpu.SemaphoreType.DMA((4, NCH)), pltpu.SemaphoreType.DMA((5,)), pltpu.SemaphoreType.DMA((4, NCH)),
                 pltpu.SemaphoreType.DMA((3,)), pltpu.SemaphoreType.DMA((26,)), pltpu.SemaphoreType.DMA((26,)),
             ],
@@ -732,7 +790,7 @@
                 vmem(NL, NR, NC), vmem(NL, NR + 8, NC), vmem(NL, NR + 16, NC), vmem(NL, NR + 16, NC),
                 vmem(9, ER, EC), *([vmem(2, ER, EC)] * 3),
                 vmem(NR, 128), vmem(NR, 128), vmem(48, NC), vmem(48, NC), vmem(24, NC), tile, *([strip] * 4), tile, *([vmem(NL, NR, 128)] * 2),
-                pltpu.SemaphoreType.DMA((4,)), pltpu.SemaphoreType.DMA((7,)), pltpu.SemaphoreType.DMA((4, NCH)),
+                pltpu.SemaphoreType.DMA((4,)), pltpu.SemaphoreType.DMA((8,)), pltpu.SemaphoreType.DMA((4, NCH)),
                 pltpu.SemaphoreType.DMA((3,)),
             ],
             compiler_params=pltpu.CompilerParams(vmem_limit_bytes=60 * 2**20),

time: 65.1 us -> 60 us (0.922)
  Pallas kernels: 64.4 us -> 59.1 us
    pallas_call x1, Pallas kernels: 39.3 us -> 34.6 us  [local_step(): pl.pallas_call(predict_kernel, name='predict', out_shape=(cube, cube, cub...]
where the time goes in v4:
time: 60 us; the launch traced here: 59.7 us
  Pallas kernels  59.1 us (98%)
  between operations  0.64 us (1%)
    pallas_call x1, Pallas kernels, local_step(): pl.pallas_call(predict_kernel, name='predict', out_shape=(cube, cube, cub...  34.6 us
    pallas_call x1, Pallas kernels, local_step(): pl.pallas_call(finish_kernel, name='finish', out_shape=(plane, plane, pla...  24.5 us

profile of v4, /device:TPU:0, one launch (start us, length us, event | category | flops | bytes accessed | tf_op | source)
XLA Modules:
  0.0 59.7 jit_solution(9859985214638008839)
XLA Ops:
  0.6 34.6 %predict.1 = (f32[20,128,512]{2,1,0:T(8,128)}, f32[20,128,512]{2,1,0:T(8,128)}, f32[20,128,512]{2,1,0:T(8,128)}, f32[20,128,512]{2,1,0:T(8,128)}, f32[9,176,640]...) custom-call(f32[20,128,512]{2,1,0:T(8,128)} %u_h.1, ...), custom_call_target="tpu_custom_call" | custom-call | tf_op jit(solution)/shard_map/predict/pallas_call | solution.py:763
  35.2 24.5 %finish.1 = (f32[128,512]{1,0:T(8,128)}, f32[128,512]{1,0:T(8,128)}, f32[128,512]{1,0:T(8,128)}, f32[20,128,512]{2,1,0:T(8,128)}, f32[20,128,512]{2,1,0:T(8,128)...) custom-call(f32[2,20]{1,0:T(2,128)} %bitcast.1, f32[20,128,512]{2,1,0:T(8,128)} %get-tuple-element.18.su_h, ...), custom_call_target="tpu_custom_call" | custom-call | tf_op jit(solution)/shard_map/finish/pallas_call | solution.py:783

commit v5 on v4

--- a/solution.py
+++ b/solution.py
@@ -184,7 +184,7 @@
 def predict_kernel(
     u_h, v_h, t_h, s_h, eta_h, tu_h, tv_h, dep_h, kmt_h,
     su_o, sv_o, tm_o, sm_o, ext_o, gts_o, gu_o, grts_o, grtn_o, grv_o, sts_o,
-    ub, vb, pb, tb, sb, su, sv, ext, ktmp, htmp, pa, pb_, pc, ga, gb, gc, pka, pkb, ga2, gb2, dup, sp, gx, prn, prs, grs, grn, sts, trn, trs, sug, vrn, fp, fsp, csp, geo, wet_g, wet_o, tot, gains, gains2,
+    ub, vb, pb, tb, sb, su, sv, ext, ktmp, htmp, pa, pb_, pc, ga, gb, gc, pka, pkb, dup, sp, gx, prn, prs, grs, grn, sts, trn, trs, sug, vrn, fp, fsp, csp, geo, wet_g, wet_o, tot, gains, gains2,
     load_sem, small_sem, out_sem, outs_sem, send_sem, recv_sem,
 ):
     col = lax.axis_index("col")
@@ -428,15 +428,6 @@
             pkb[rows(t - 1), :] = even_odd(north(flux, corner_w), d * d + turn(g, -81))
         corner_w = flux
 
-    def spread(i):
-        for j in range(4):
-            at = rows(4 * i + j)
-            a, b = pka[at, :], pkb[at, :]
-            for k in range(NL):
-                ga2[k, at, :] = unpack(a, 0, k)
-                gb2[k, at, :] = unpack(b, 0, k)
-
-    loop(0, STRIPS // 4, spread)
     for k in range(NL):
         for i, ref in enumerate((ub, vb)):
             ghost_row(ref, k, 7, grs, i)
@@ -457,8 +448,9 @@
     def tendency(i):
         r = STRIPS - 1 - i
         at = rows(r)
+        near, far = pka[at, :], pkb[at, :]
         for k in range(NL):
-            ghost = ga2[k, at, :]
+            ghost = unpack(near, 0, k)
             u, p, f_s, c = corner(r, k, ghost)
             f = north(f_s, fsp[k])
             c_n = north(c, csp[k])
@@ -471,7 +463,7 @@
         k_u, k_v, dz_u, dz_v = (geo[i, rows(r, 8), :] for i in (KU, KV, DU, DV))
         sum_u = sum_v = jnp.zeros((8, NC), F32)
         for k in range(NL):
-            ghost = gb2[k, at, :]
+            ghost = unpack(far, 0, k)
             t_u = su[k, at, :] - east_of(dup[k], ghost)
             t_v = sv[k, at, :] + west_of(fp[k], ghost)
             u = jnp.where(k_u > k, ub[k, rows(r, 8), :] + t_u, ZERO)
@@ -695,31 +687,24 @@
         g = gts[rows(r), :]
         pkt[rows(r), :] = even_odd(turn(uc * (g + turn(sts[rows(r), :], -1)), 1), turn(g, -1))
 
-    def spread(i):
-        for j in range(4):
-            at = rows(4 * i + j)
-            g = pkt[at, :]
-            for k in range(NL):
-                tg[k, at, :] = unpack(g, 0, k)
-                sg[k, at, :] = unpack(g, 1, k)
-
-    loop(0, STRIPS // 4, spread)
-
     def advect(r):
         kc, k_u, k_v, d_u, d_v = strip(r)
+        edges = pkt[rows(r), :]
         for k in range(NL):
             vc, t, y_t, s, y_s = flux_y(r, k, k_v, d_v)
             vb[k, rows(r, 8), :] = vc
             uc = jnp.where(k_u > k, ub[k, rows(r), :] + d_u, ZERO)
             ub[k, rows(r), :] = uc
-            for ref, ghost, prev, keep, x, y in ((tb, tg, fpt, fxt, t, y_t), (sb, sg, fps, fxs, s, y_s)):
-                fx = uc * (x + east_of(x, ghost[k, rows(r), :]))
+            for slot, (ref, edge, prev, keep, x, y) in enumerate(((tb, tg, fpt, fxt, t, y_t), (sb, sg, fps, fxs, s, y_s))):
+                ghost = unpack(edges, slot, k)
+                edge[k] = ghost
+                fx = uc * (x + east_of(x, ghost))
                 keep[k] = fx
                 ref[k, rows(r, 8), :] = x - HALF_DT * (fx + (y - south(y, prev[k])))
                 prev[k] = y
         for k in range(NL):
-            for ref, ghost, keep in ((tb, tg, fxt), (sb, sg, fxs)):
-                x = ref[k, rows(r, 8), :] + HALF_DT * west_of(keep[k], ghost[k, rows(r), :])
+            for ref, edge, keep in ((tb, tg, fxt), (sb, sg, fxs)):
+                x = ref[k, rows(r, 8), :] + HALF_DT * west_of(keep[k], edge[k])
                 ref[k, rows(r, 8), :] = jnp.where(kc > k, x, ZERO)
 
     def out_copy(i, c):
@@ -734,7 +719,7 @@
         for i in range(4):
             out_copy(i, c).start()
 
-    loop(0, NCH, advect_chunk, PAIR)
+    loop(0, NCH, advect_chunk)
 
     def drain(c):
         for i in range(4):
@@ -772,7 +757,7 @@
             scratch_shapes=[
                 *([vmem(NL, NR + 16, NC)] * 3), *([vmem(NL, NR, NC)] * 4),
                 vmem(9, ER, EC), pltpu.VMEM((NR, NC), jnp.int32), vmem(NR, NC),
-                *([tile] * 3), *([ghost] * 3), vmem(NR + 8, 128), tile, *([vmem(NL, NR, 128)] * 2), strip, *([vmem(NR + 16, 128)] * 2),
+                *([tile] * 3), *([ghost] * 3), vmem(NR + 8, 128), tile, strip, *([vmem(NR + 16, 128)] * 2),
                 vmem(48, NC), vmem(72, NC), vmem(48, NC), vmem(72, NC),
                 tile, vmem(48, NC), vmem(48, NC), tile, vmem(24, NC), *([strip] * 3), vmem(4, NR + 16, NC), *([vmem(NR + 16, 128)] * 2), vmem(2, NR, NC), strip, strip,
                 pltpu.SemaphoreType.DMA((4, NCH)), pltpu.SemaphoreType.DMA((5,)), pltpu.SemaphoreType.DMA((4, NCH)),
@@ -789,7 +774,7 @@
             scratch_shapes=[
                 vmem(NL, NR, NC), vmem(NL, NR + 8, NC), vmem(NL, NR + 16, NC), vmem(NL, NR + 16, NC),
                 vmem(9, ER, EC), *([vmem(2, ER, EC)] * 3),
-                vmem(NR, 128), vmem(NR, 128), vmem(48, NC), vmem(48, NC), vmem(24, NC), tile, *([strip] * 4), tile, *([vmem(NL, NR, 128)] * 2),
+                vmem(NR, 128), vmem(NR, 128), vmem(48, NC), vmem(48, NC), vmem(24, NC), tile, *([strip] * 4), tile, *([vmem(NL, 8, 128)] * 2),
                 pltpu.SemaphoreType.DMA((4,)), pltpu.SemaphoreType.DMA((8,)), pltpu.SemaphoreType.DMA((4, NCH)),
                 pltpu.SemaphoreType.DMA((3,)),
             ],

time: 60 us -> 59 us (0.983)
  Pallas kernels: 59.1 us -> 58 us
    pallas_call x1, Pallas kernels: 24.5 us -> 23.6 us  [local_step(): pl.pallas_call(finish_kernel, name='finish', out_shape=(plane, plane, pla...]
where the time goes in v5:
time: 59 us; the launch traced here: 58.7 us
  Pallas kernels  58 us (98%)
  between operations  0.64 us (1%)
    pallas_call x1, Pallas kernels, local_step(): pl.pallas_call(predict_kernel, name='predict', out_shape=(cube, cube, cub...  34.5 us
    pallas_call x1, Pallas kernels, local_step(): pl.pallas_call(finish_kernel, name='finish', out_shape=(plane, plane, pla...  23.6 us

profile of v5, /device:TPU:0, one launch (start us, length us, event | category | flops | bytes accessed | tf_op | source)
XLA Modules:
  0.0 58.7 jit_solution(5488609648981555026)
XLA Ops:
  0.6 34.5 %predict.1 = (f32[20,128,512]{2,1,0:T(8,128)}, f32[20,128,512]{2,1,0:T(8,128)}, f32[20,128,512]{2,1,0:T(8,128)}, f32[20,128,512]{2,1,0:T(8,128)}, f32[9,176,640]...) custom-call(f32[20,128,512]{2,1,0:T(8,128)} %u_h.1, ...), custom_call_target="tpu_custom_call" | custom-call | tf_op jit(solution)/shard_map/predict/pallas_call | solution.py:748
  35.1 23.6 %finish.1 = (f32[128,512]{1,0:T(8,128)}, f32[128,512]{1,0:T(8,128)}, f32[128,512]{1,0:T(8,128)}, f32[20,128,512]{2,1,0:T(8,128)}, f32[20,128,512]{2,1,0:T(8,128)...) custom-call(f32[2,20]{1,0:T(2,128)} %bitcast.1, f32[20,128,512]{2,1,0:T(8,128)} %get-tuple-element.18.su_h, ...), custom_call_target="tpu_custom_call" | custom-call | tf_op jit(solution)/shard_map/finish/pallas_call | solution.py:768
